TPU v7x, 32 devices: a whole 2x2x4 slice. The times are simulated.
32 devices in a mesh: space: 8 (over z, y), tm: 4 (over x, core).
Axes of the slice: x: 2, y: 2, z: 4, core: 2. Of those that a mesh axis runs over, the one named last changes fastest.
Arguments:
- innovations: bfloat16 [12, 32, 768, 1536], P('tm', None, 'space'), may hold values from -6 to 6
- obs_counts: int32 [12, 192, 384], P('tm', 'space'), may hold values from 0 to 3
- diffusion: float32 [32, 192, 384], P(None, 'space'), may hold values from 0.01 to 0.1
- courant: float32 [32, 192, 384], P(None, 'space'), may hold values from 0 to 0.4
Outputs:
- increment: float32 [32, 768, 1536], P('tm', 'space')
- residual: float32 [32, 192, 384], P('tm', 'space')
All inputs are finite; a program needn't handle non-finite values.
Results may differ from a plain program's by a relative error of at most 0.0003.
Values sent between devices are 32-bit elements; how exact they have to be, the bound alone decides.
A program may use at most 384 MiB of HBM per device.

v0:
```python
import functools

import jax
import jax.numpy as jnp
from jax import lax
from jax.experimental import pallas as pl
from jax.experimental.pallas import tpu as pltpu
from jax.sharding import PartitionSpec as P

ITERS = 3
F32 = jnp.float32
BF16 = jnp.bfloat16
MESH = pl.DeviceIdType.MESH
BLOCK = 4
ROWS = 4
COARSE = 4


def restrict_kernel(inn, counts, diff, cour, forcing, weights, diff_t, cour_t, summed, turned):
    levels, fine_rows, fine_cols = inn.shape[1:]
    rows, cols = fine_rows // COARSE, fine_cols // COARSE
    weights[0] = counts[0].astype(F32)
    wide = 128 * COARSE
    pick = jnp.where(
        lax.broadcasted_iota(jnp.int32, (wide, 128), 0) // COARSE
        == lax.broadcasted_iota(jnp.int32, (wide, 128), 1),
        1.0 / (COARSE * COARSE),
        0.0,
    ).astype(BF16)
    for part in range(cols // 128):
        block = inn[0, :, :, part * wide : (part + 1) * wide].reshape(levels * fine_rows, wide)
        summed[part] = jnp.dot(block, pick, preferred_element_type=F32)
    for part in range(cols // 128):
        at = slice(part * 128, (part + 1) * 128)
        scale = weights[0, :, at]
        for level in range(levels):
            total = summed[part, pl.ds(level * fine_rows, rows, stride=COARSE), :]
            for sub in range(1, COARSE):
                total += summed[part, pl.ds(level * fine_rows + sub, rows, stride=COARSE), :]
            turned[part, pl.ds(level, rows, stride=levels), :] = total * scale
        forcing[0, 0, :, :, at] = turned[part].reshape(rows, levels, 128)

    @pl.when(pl.program_id(1) == 0)
    def _():
        for row in range(rows):
            diff_t[0, row] = diff[:, row, :]
            cour_t[0, row] = cour[:, row, :]


def restrict_call(innovations, obs_counts, diffusion, courant, sections):
    steps, levels, fine_rows, fine_cols = innovations.shape
    part = levels // sections
    rows, cols = fine_rows // COARSE, fine_cols // COARSE
    field = pl.BlockSpec((part, rows, cols), lambda g, t: (g, 0, 0))
    field_t = pl.BlockSpec((1, rows, part, cols), lambda g, t: (g, 0, 0, 0))
    step = pl.BlockSpec((1, rows, cols), lambda g, t: (t, 0, 0))
    return pl.pallas_call(
        restrict_kernel,
        grid=(sections, steps),
        in_specs=[
            pl.BlockSpec((1, part, fine_rows, fine_cols), lambda g, t: (t, g, 0, 0)),
            step,
            field,
            field,
        ],
        out_specs=[
            pl.BlockSpec((1, 1, rows, part, cols), lambda g, t: (g, t, 0, 0, 0)),
            step,
            field_t,
            field_t,
        ],
        out_shape=[
            jax.ShapeDtypeStruct((sections, steps, rows, part, cols), F32),
            jax.ShapeDtypeStruct((steps, rows, cols), F32),
            jax.ShapeDtypeStruct((sections, rows, part, cols), F32),
            jax.ShapeDtypeStruct((sections, rows, part, cols), F32),
        ],
        scratch_shapes=[
            pltpu.VMEM((cols // 128, part * fine_rows, 128), F32),
            pltpu.VMEM((cols // 128, part * rows, 128), F32),
        ],
        compiler_params=pltpu.CompilerParams(vmem_limit_bytes=48 * 2**20),
        name="restrict",
    )(innovations, obs_counts, diffusion, courant)


def expand_kernel(control, residual, increment, residual_out, held, repeated):
    rows, cols = residual_out.shape[1:]
    part = control.shape[0] // rows
    level = pl.program_id(0)
    wide = 128 * COARSE

    @pl.when(level == 0)
    def _():
        for piece in range(cols // 128):
            held[0, piece] = control[:, piece * 128 : (piece + 1) * 128]
            held[1, piece] = residual[:, piece * 128 : (piece + 1) * 128]

    pick = jnp.where(
        lax.broadcasted_iota(jnp.int32, (128, wide), 1) // COARSE
        == lax.broadcasted_iota(jnp.int32, (128, wide), 0),
        1.0,
        0.0,
    ).astype(BF16)
    for piece in range(cols // 128):
        at = pl.ds(level, rows, stride=part)
        residual_out[0, :, piece * 128 : (piece + 1) * 128] = held[1, piece, at, :]
        values = held[0, piece, at, :]
        for sub in range(COARSE):
            repeated[piece, pl.ds(sub, rows, stride=COARSE), :] = values
        rest = repeated[piece]
        total = None
        for _ in range(3):
            head = rest.astype(BF16)
            rest = rest - head.astype(F32)
            spread = jnp.dot(head, pick, preferred_element_type=F32)
            total = spread if total is None else total + spread
        increment[0, :, piece * wide : (piece + 1) * wide] = total


def expand_call(control, residual):
    rows, part, cols = control.shape
    whole = pl.BlockSpec((rows * part, cols), lambda l: (0, 0))
    return pl.pallas_call(
        expand_kernel,
        grid=(part,),
        in_specs=[whole, whole],
        out_specs=[
            pl.BlockSpec((1, rows * COARSE, cols * COARSE), lambda l: (l, 0, 0)),
            pl.BlockSpec((1, rows, cols), lambda l: (l, 0, 0)),
        ],
        out_shape=[
            jax.ShapeDtypeStruct((part, rows * COARSE, cols * COARSE), F32),
            jax.ShapeDtypeStruct((part, rows, cols), F32),
        ],
        scratch_shapes=[
            pltpu.VMEM((2, cols // 128, rows * part, 128), F32),
            pltpu.VMEM((cols // 128, rows * COARSE, 128), F32),
        ],
        compiler_params=pltpu.CompilerParams(vmem_limit_bytes=32 * 2**20),
        name="expand",
    )(control.reshape(rows * part, cols), residual.reshape(rows * part, cols))


def solve_kernel(
    n_space,
    n_tm,
    forcing,
    weights,
    diff,
    cour,
    control,
    residual,
    co_a,
    co_b,
    co_d,
    states,
    wts,
    lam,
    direction,
    p_send,
    p_recv,
    w_recv,
    edge_recv,
    halo_recv,
    send_buf,
    swap_recv,
    red_src,
    red_tm,
    red_space,
    p_sems,
    w_sems,
    edge_sems,
    halo_sems,
    swap_sems,
    red_tm_sems,
    red_space_sems,
):
    steps, rows, part, cols = forcing.shape[1:]
    total_steps = steps * n_tm
    halo = total_steps - 1
    pad = halo + 1
    place = lax.axis_index("space")
    section = lax.axis_index("tm")
    above, below = place - 1, place + 1
    has_above, has_below = place > 0, place < n_space - 1
    own = pl.ds(pad, rows)
    top, bottom = pl.ds(pad - halo, halo), pl.ds(pad + rows, halo)

    def over_rows(low, count, fn):
        blocks = (count + BLOCK - 1) // BLOCK

        def one(block, carry):
            fn(low + block * BLOCK)
            return carry

        lax.fori_loop(0, blocks, one, 0)

    def by_block(count, fn, carry=0):
        full = count // ROWS

        def one(block, carry):
            return fn(block * ROWS, ROWS, carry)

        if full:
            carry = lax.fori_loop(0, full, one, carry)
        if count % ROWS:
            carry = fn(full * ROWS, count % ROWS, carry)
        return carry

    def clear(ref, count, first=0):
        def one(row, size, carry):
            ref[pl.ds(first + row, size)] = jnp.zeros((size, *ref.shape[1:]), F32)
            return carry

        by_block(count, one)

    def to(axis, peer):
        return {"device_id": {axis: peer}, "device_id_type": MESH}

    edge_recv[...] = jnp.zeros_like(edge_recv)
    for side in range(2):
        for k in range(2):
            clear(halo_recv.at[side, k], halo)
        for k in range(swap_recv.shape[0]):
            clear(swap_recv.at[k, side], halo)

    tm_peers = [lax.rem(section + k, n_tm) for k in range(1, n_tm)]
    space_peers = [lax.rem(place + k, n_space) for k in range(1, n_space)]
    barrier = pltpu.get_barrier_semaphore()
    for peer in tm_peers:
        pl.semaphore_signal(barrier, inc=1, **to("tm", peer))
    for peer in space_peers:
        pl.semaphore_signal(barrier, inc=1, **to("space", peer))
    pl.semaphore_wait(barrier, n_tm - 1 + n_space - 1)

    def pair(up_src, down_src, up_dst, down_dst, sems):
        up = pltpu.make_async_remote_copy(
            src_ref=up_src, dst_ref=up_dst, send_sem=sems.at[0, 0], recv_sem=sems.at[1, 0], **to("space", above)
        )
        down = pltpu.make_async_remote_copy(
            src_ref=down_src, dst_ref=down_dst, send_sem=sems.at[0, 1], recv_sem=sems.at[1, 1], **to("space", below)
        )
        return [(has_above, has_below, up), (has_below, has_above, down)]

    def start(copies):
        for sends, _, copy in copies:
            pl.when(sends)(copy.start)

    def finish(copies):
        for sends, receives, copy in copies:
            pl.when(sends)(copy.wait_send)
            pl.when(receives)(copy.wait_recv)

    edge_copies = []
    for k, field in enumerate((diff, cour)):
        edge_copies += pair(
            field.at[:, pl.ds(0, 1)],
            field.at[:, pl.ds(rows - 1, 1)],
            edge_recv.at[1, k],
            edge_recv.at[0, k],
            edge_sems.at[k],
        )
    start(edge_copies)
    w_copies = []
    for k, peer in enumerate(tm_peers):
        w_copies.append(
            pltpu.make_async_remote_copy(
                src_ref=weights,
                dst_ref=w_recv.at[section],
                send_sem=w_sems.at[0, k],
                recv_sem=w_sems.at[1, section],
                **to("tm", peer),
            )
        )
    for copy in w_copies:
        copy.start()
    halo_copies = []
    for k, field in enumerate((diff, cour)):
        halo_copies += pair(
            field.at[section, pl.ds(0, halo)],
            field.at[section, pl.ds(rows - halo, halo)],
            halo_recv.at[1, k],
            halo_recv.at[0, k],
            halo_sems.at[k],
        )
    start(halo_copies)

    clear(co_a, co_a.shape[0])
    clear(co_b, co_b.shape[0])
    clear(co_d, co_d.shape[0])

    def put_coefs(row, d, c, inside=None):
        a = 1.0 - 4.0 * d - c
        b = d + c
        if inside is not None:
            a = jnp.where(inside, a, 0.0)
        co_a[row] = a
        co_b[row] = b
        co_d[row] = d

    def adjoint_block(slot, low):
        here = pl.ds(low, BLOCK)
        around = pl.ds(low - 1, BLOCK + 2)
        y = lam[slot, around]
        s = co_d[around] * y
        yc, sc = y[1:-1], s[1:-1]
        return (
            co_a[here] * yc
            + (s[:-2] + s[2:])
            + pltpu.roll(sc, 1, 2)
            + pltpu.roll(co_b[here] * yc, cols - 1, 2)
        )

    def adjoint_step(slot, grown):
        def fn(low):
            lam[1 - slot, pl.ds(low, BLOCK)] = adjoint_block(slot, low)

        over_rows(pad - grown, rows + 2 * grown, fn)

    def add_rows(slot, at, term, count):
        def fn(row, size, carry):
            here = pl.ds(at + row, size)
            lam[slot, here] = lam[slot, here] + term[pl.ds(row, size)]
            return carry

        by_block(count, fn)

    def clear_lam():
        clear(lam.at[0], lam.shape[1])
        clear(lam.at[1], lam.shape[1])

    finish(edge_copies)
    reach = steps - 1
    p_copies = []
    for turn in range(n_tm):
        group = lax.rem(section + turn + 1, n_tm)

        def fill(row, size, carry, group=group):
            here = pl.ds(row, size)
            put_coefs(pl.ds(pad + row, size), diff[group, here], cour[group, here])
            return carry

        by_block(rows, fill)
        put_coefs(pad - 1, edge_recv[0, 0, group, 0], edge_recv[0, 1, group, 0], has_above)
        put_coefs(pad + rows, edge_recv[1, 0, group, 0], edge_recv[1, 1, group, 0], has_below)
        clear_lam()
        slot = 0
        add_rows(slot, pad, forcing.at[group, steps - 1], rows)
        for k in range(1, steps):
            adjoint_step(slot, k)
            slot = 1 - slot
            add_rows(slot, pad, forcing.at[group, steps - 1 - k], rows)
        target = p_send.at[turn] if turn < n_tm - 1 else p_recv.at[section]

        def keep(row, size, carry, slot=slot, target=target):
            target[pl.ds(row, size)] = lam[slot, pl.ds(pad - reach + row, size)]
            return carry

        by_block(rows + 2 * reach, keep)
        if turn < n_tm - 1:
            copy = pltpu.make_async_remote_copy(
                src_ref=p_send.at[turn],
                dst_ref=p_recv.at[section],
                send_sem=p_sems.at[0, turn],
                recv_sem=p_sems.at[1, section],
                **to("tm", group),
            )
            copy.start()
            p_copies.append(copy)

    for t in range(total_steps):
        clear(states.at[t], states.shape[1] - pad - rows, pad + rows)
        clear(wts.at[t], pad)
        clear(wts.at[t], wts.shape[1] - pad - rows, pad + rows)

    def from_peer(k, ref_src, ref_dst, sems):
        peer = tm_peers[k]
        return pltpu.make_async_remote_copy(
            src_ref=ref_src, dst_ref=ref_dst.at[peer], send_sem=sems.at[0, k], recv_sem=sems.at[1, peer], **to("tm", peer)
        )

    for k in range(n_tm - 1):
        w_copies[k].wait_send()
        from_peer(k, weights, w_recv, w_sems).wait_recv()
    w_recv[section] = weights[...]

    def spread_weights(row, carry):
        for t in range(total_steps):
            line = w_recv[t // steps, t % steps, pl.ds(row, 1), :]
            wts[t, pad + row] = jnp.broadcast_to(line, (part, cols))
        return carry

    lax.fori_loop(0, rows, spread_weights, 0)

    finish(halo_copies)

    def fill_halo(row, size, carry):
        here = pl.ds(row, size)
        put_coefs(pl.ds(pad - halo + row, size), halo_recv[0, 0, here], halo_recv[0, 1, here], has_above)
        put_coefs(pl.ds(pad + rows + row, size), halo_recv[1, 0, here], halo_recv[1, 1, here], has_below)
        return carry

    by_block(halo, fill_halo)

    for k in range(n_tm - 1):
        p_copies[k].wait_send()
        from_peer(k, p_send.at[k], p_recv, p_sems).wait_recv()
    clear_lam()
    slot = 0
    grown = reach
    add_rows(slot, pad - reach, p_recv.at[n_tm - 1], rows + 2 * reach)
    for other in range(n_tm - 2, -1, -1):
        for _ in range(steps):
            grown += 1
            adjoint_step(slot, grown)
            slot = 1 - slot
        add_rows(slot, pad - reach, p_recv.at[other], rows + 2 * reach)

    def scatter(slot, k):
        copies = pair(lam.at[slot, top], lam.at[slot, bottom], swap_recv.at[k, 1], swap_recv.at[k, 0], swap_sems.at[k])
        start(copies)
        return copies

    def add_scattered(slot, k):
        add_rows(slot, pad, swap_recv.at[k, 0], halo)
        add_rows(slot, pad + rows - halo, swap_recv.at[k, 1], halo)

    def gather(k):
        copies = pair(
            residual.at[pl.ds(0, halo)],
            residual.at[pl.ds(rows - halo, halo)],
            swap_recv.at[k, 1],
            swap_recv.at[k, 0],
            swap_sems.at[k],
        )
        start(copies)
        return copies

    def reduce_over(axis, me, peers, count, tile, k, src, slots, sems):
        src[...] = tile
        slots[me] = tile
        copies = []
        for j, peer in enumerate(peers):
            copies.append(
                pltpu.make_async_remote_copy(
                    src_ref=src,
                    dst_ref=slots.at[me],
                    send_sem=sems.at[0, j],
                    recv_sem=sems.at[1, me],
                    **to(axis, peer),
                )
            )
        for copy in copies:
            copy.start()
        for j, peer in enumerate(peers):
            copies[j].wait_send()
            pltpu.make_async_remote_copy(
                src_ref=src,
                dst_ref=slots.at[peer],
                send_sem=sems.at[0, j],
                recv_sem=sems.at[1, peer],
                **to(axis, peer),
            ).wait_recv()
        total = slots[0]
        for j in range(1, count):
            total = total + slots[j]
        return total

    def reduce_all(partial, k):
        tile = partial[:, :128]
        for piece in range(1, cols // 128):
            tile = tile + partial[:, piece * 128 : (piece + 1) * 128]
        tile = reduce_over("tm", section, tm_peers, n_tm, tile, k, red_src.at[k, 0], red_tm.at[k], red_tm_sems.at[k])
        tile = reduce_over(
            "space", place, space_peers, n_space, tile, k, red_src.at[k, 1], red_space.at[k], red_space_sems.at[k]
        )
        return jnp.sum(jnp.sum(tile, axis=0, keepdims=True), axis=1, keepdims=True)

    none = jnp.zeros((part, cols), F32)
    copies = scatter(slot, 0)
    finish(copies)
    add_scattered(slot, 0)

    def take_rhs(row, size, acc, slot=slot):
        value = lam[slot, pl.ds(pad + row, size)]
        residual[pl.ds(row, size)] = value
        control[pl.ds(row, size)] = jnp.zeros_like(value)
        return acc + jnp.sum(value * value, axis=0)

    partial = by_block(rows, take_rhs, none)
    swap = 1
    red = 0
    norm_now = None
    for iter_no in range(ITERS):
        copies = gather(swap)
        norm_next = reduce_all(partial, red)
        red += 1
        finish(copies)
        first = iter_no == 0
        beta = None if first else norm_next / norm_now
        norm_now = norm_next

        def new_direction(here, value, beta=beta):
            if beta is not None:
                value = value + beta.reshape(1, 1, 1) * direction[here]
            direction[here] = value
            states[0, here] = value
            return value

        def own_direction(row, size, acc, new=new_direction):
            value = new(pl.ds(pad + row, size), residual[pl.ds(row, size)])
            return acc + jnp.sum(value * value, axis=0)

        def halo_direction(row, size, carry, new=new_direction, swap=swap):
            here = pl.ds(row, size)
            new(pl.ds(pad - halo + row, size), swap_recv[swap, 0, here])
            new(pl.ds(pad + rows + row, size), swap_recv[swap, 1, here])
            return carry

        squares = by_block(rows, own_direction, none)
        by_block(halo, halo_direction)
        swap += 1
        clear_lam()

        def forward_step(t, carry):
            def fn(low):
                here = pl.ds(low, BLOCK)
                x = states[t - 1, pl.ds(low - 1, BLOCK + 2)]
                xc = x[1:-1]
                states[t, here] = (
                    co_a[here] * xc
                    + co_d[here] * (x[:-2] + x[2:] + pltpu.roll(xc, cols - 1, 2))
                    + co_b[here] * pltpu.roll(xc, 1, 2)
                )

            over_rows(pad - halo + t, rows + 2 * (halo - t), fn)
            return carry

        lax.fori_loop(1, total_steps, forward_step, 0)

        def last_term(row, size, acc):
            here = pl.ds(pad + row, size)
            x = states[total_steps - 1, here]
            g = wts[total_steps - 1, here] * x
            lam[0, here] = g
            return acc + jnp.sum(g * x, axis=0)

        squares = by_block(rows, last_term, squares)

        def backward_step(k, acc):
            t = total_steps - 2 - k
            slot = lax.rem(k, 2)
            grown = halo - t

            def one(block, acc):
                low = pad - grown + block * BLOCK
                here = pl.ds(low, BLOCK)
                x = states[t, here]
                g = wts[t, here] * x
                lam[1 - slot, here] = adjoint_block(slot, low) + g
                return acc + jnp.sum(g * x, axis=0)

            return lax.fori_loop(0, (rows + 2 * grown + BLOCK - 1) // BLOCK, one, acc)

        squares = lax.fori_loop(0, total_steps - 1, backward_step, squares)
        slot = (total_steps - 1) % 2
        copies = scatter(slot, swap)
        step_len = norm_now / reduce_all(squares, red)
        red += 1
        finish(copies)
        add_scattered(slot, swap)
        swap += 1

        def update(row, size, acc, slot=slot, step_len=step_len.reshape(1, 1, 1)):
            here, ext = pl.ds(row, size), pl.ds(pad + row, size)
            d = direction[ext]
            control[here] = control[here] + step_len * d
            value = residual[here] - step_len * (d + lam[slot, ext])
            residual[here] = value
            return acc + jnp.sum(value * value, axis=0)

        partial = by_block(rows, update, none)


def solve_call(forcing, weights, diff_t, cour_t, n_space, n_tm):
    sections, steps, rows, part, cols = forcing.shape
    total_steps = steps * n_tm
    halo = total_steps - 1
    ext = rows + 2 * (halo + 1) + BLOCK
    p_rows = rows + 2 * (steps - 1)
    swaps = 1 + 2 * ITERS
    reds = 2 * ITERS
    vmem = pl.BlockSpec(memory_space=pltpu.VMEM)
    row = (part, cols)
    dma = pltpu.SemaphoreType.DMA
    return pl.pallas_call(
        functools.partial(solve_kernel, n_space, n_tm),
        out_shape=[jax.ShapeDtypeStruct((rows, *row), F32)] * 2,
        in_specs=[vmem] * 4,
        out_specs=[vmem] * 2,
        scratch_shapes=[
            pltpu.VMEM((ext, *row), F32),
            pltpu.VMEM((ext, *row), F32),
            pltpu.VMEM((ext, *row), F32),
            pltpu.VMEM((total_steps, ext, *row), F32),
            pltpu.VMEM((total_steps, ext, *row), F32),
            pltpu.VMEM((2, ext, *row), F32),
            pltpu.VMEM((ext, *row), F32),
            pltpu.VMEM((n_tm - 1, p_rows, *row), F32),
            pltpu.VMEM((n_tm, p_rows, *row), F32),
            pltpu.VMEM((n_tm, steps, rows, cols), F32),
            pltpu.VMEM((2, 2, n_tm, 1, *row), F32),
            pltpu.VMEM((2, 2, halo, *row), F32),
            pltpu.VMEM((1, 8, 128), F32),
            pltpu.VMEM((swaps, 2, halo, *row), F32),
            pltpu.VMEM((reds, 2, part, 128), F32),
            pltpu.VMEM((reds, n_tm, part, 128), F32),
            pltpu.VMEM((reds, n_space, part, 128), F32),
            dma((2, n_tm)),
            dma((2, n_tm)),
            dma((2, 2, 2)),
            dma((2, 2, 2)),
            dma((swaps, 2, 2)),
            dma((reds, 2, n_tm)),
            dma((reds, 2, n_space)),
        ],
        compiler_params=pltpu.CompilerParams(
            collective_id=0, has_side_effects=True, vmem_limit_bytes=60 * 2**20
        ),
        name="solve",
    )(forcing, weights, diff_t, cour_t)


def padded_2(cells, sides, width):
    for axis, dim in sides:
        count = lax.axis_size(axis)
        ends = count - 1
        head = lax.slice_in_dim(cells, 0, width, axis=dim)
        tail = lax.slice_in_dim(cells, cells.shape[dim] - width, cells.shape[dim], axis=dim)
        cells = jnp.concatenate(
            [
                lax.ppermute(tail, axis, [(i, (i + 1) % count) for i in range(ends)]),
                cells,
                lax.ppermute(head, axis, [((i + 1) % count, i) for i in range(ends)]),
            ],
            axis=dim,
        )
    return cells


def laplace_rows(padded, state_field):
    return (
        padded[:, 2:, :]
        + padded[:, :-2, :]
        + jnp.roll(state_field, 1, 2)
        + jnp.roll(state_field, -1, 2)
        - 4.0 * state_field
    )


def tangent(state_field, diffusion, courant):
    padded = padded_2(state_field, (("space", 1),), 1)
    return (
        state_field
        + diffusion * laplace_rows(padded, state_field)
        - courant * (state_field - jnp.roll(state_field, 1, 2))
    )


def adjoint(state_field, diffusion, courant):
    carried = courant * state_field
    spread = diffusion * state_field
    padded = padded_2(spread, (("space", 1),), 1)
    return state_field + laplace_rows(padded, spread) - carried + jnp.roll(carried, -1, 2)


def level_squares(residual):
    return lax.psum(jnp.sum(residual * residual), ("space", "tm"))


def level_curve(direction, hessian_image):
    return lax.psum(jnp.sum(direction * hessian_image), ("space", "tm"))


def solve_inner(rhs_field, hessian_part, norm_fn, curve_fn):
    control = jnp.zeros_like(rhs_field)
    residual = rhs_field
    direction = rhs_field
    norm_now = norm_fn(residual)
    for iter_no in range(ITERS):
        hessian_image = direction + hessian_part(direction)
        step_len = norm_now / curve_fn(direction, hessian_image)
        control = control + step_len * direction
        residual = residual - step_len * hessian_image
        if iter_no + 1 < ITERS:
            norm_next = norm_fn(residual)
            direction = residual + norm_next / norm_now * direction
            norm_now = norm_next
    return (control, residual)


def on_device(innovations, obs_counts, diffusion, courant):
    step_dev = obs_counts.shape[0]
    n_sections = lax.axis_size("tm")
    section_pos = lax.axis_index("tm")
    total_steps = step_dev * n_sections
    weights = obs_counts.astype(jnp.float32)[:, None]
    levels, fine_rows, fine_cols = (
        innovations.shape[1],
        innovations.shape[2],
        innovations.shape[3],
    )
    lev_part = levels // n_sections
    rows, cols = fine_rows // COARSE, fine_cols // COARSE
    if lev_part == 8 and rows % 8 == 0 and rows >= total_steps - 1 and cols % 128 == 0:
        forced = restrict_call(innovations, obs_counts, diffusion, courant, n_sections)
        solved = solve_call(*forced, lax.axis_size("space"), n_sections)
        return tuple(expand_call(*solved))
    blocks = innovations.reshape(step_dev, levels, fine_rows // 4, 4, fine_cols // 4, 4).astype(
        jnp.float32
    )
    forcing = weights * jnp.mean(blocks, axis=(3, 5))
    all_weights = lax.all_gather(obs_counts, "tm", axis=0, tiled=True).astype(jnp.float32)[:, None]
    all_forcing = lax.all_to_all(forcing, "tm", split_axis=1, concat_axis=0, tiled=True)
    diff_part = lax.dynamic_slice_in_dim(diffusion, section_pos * lev_part, lev_part, 0)
    cour_part = lax.dynamic_slice_in_dim(courant, section_pos * lev_part, lev_part, 0)

    def level_back(terms):
        current = terms[total_steps - 1]
        for step_no in range(total_steps - 2, -1, -1):
            current = terms[step_no] + adjoint(current, diff_part, cour_part)
        return current

    def level_hess(state_field):
        records = []
        for step_no in range(total_steps):
            records.append(all_weights[step_no] * state_field)
            if step_no + 1 < total_steps:
                state_field = tangent(state_field, diff_part, cour_part)
        return level_back(jnp.stack(records))

    control, residual = solve_inner(level_back(all_forcing), level_hess, level_squares, level_curve)
    increment = jnp.repeat(jnp.repeat(control, 4, axis=1), 4, axis=2)
    return (increment, residual)


def solution(mesh):
    placed = (
        P("tm", None, "space", None),
        P("tm", "space", None),
        P(None, "space", None),
        P(None, "space", None),
    )
    return jax.shard_map(
        on_device,
        mesh=mesh,
        in_specs=placed,
        out_specs=(P("tm", "space", None), P("tm", "space", None)),
        check_vma=False,
    )
```

profile of v0, /device:TPU:0, one launch (start us, length us, event | category | flops | bytes accessed | tf_op | source)
XLA Modules:
  0.0 192.6 jit_solution(17209183870591709324)
XLA Ops:
  0.6 0.0 copy-start
  0.6 1.3 copy-done
  1.9 0.0 copy-start.1
  1.9 1.3 copy-done.1
  3.2 0.0 copy-start.6
  3.2 0.9 copy-done.6
  4.1 18.8 %restrict.1 = (f32[4,3,24,8,384]{4,3,2,1,0:T(8,128)}, f32[3,24,384]{2,1,0:T(8,128)S(1)}, f32[4,24,8,384]{3,2,1,0:T(8,128)S(1)}, f32[4,24,8,384]{3,2,1,0:T(8,128)S(1)}) custom-call(bf16[3,32,96,1536]{3,2,1,0:T(8,128)(2,1)} %inn.1, s32[3,24,384]{2,1,0:T(8,128)S(1)} %copy-done.6, f32[32,24,384]{2,1,0:T(8,128)S(1)} %copy-done, f32[32,24,384]{2,1,0:T(8,128)S(1)} %copy-done.1), custom_call_target="tpu_custom_call" | custom-call | tf_op jit(solution)/shard_map/restrict/pallas_call | solution.py:57
  22.8 0.0 copy-start.2
  22.8 1.0 copy-done.2
  23.9 0.0 copy-start.3
  23.9 1.0 copy-done.3
  24.9 0.0 copy-start.7
  24.9 0.6 copy-done.7
  25.5 159.8 %solve.1 = (f32[24,8,384]{2,1,0:T(8,128)}, f32[24,8,384]{2,1,0:T(8,128)}) custom-call(f32[4,3,24,8,384]{4,3,2,1,0:T(8,128)} %get-tuple-element.8.forcing, f32[3,24,384]{2,1,0:T(8,128)} %copy-done.7, f32[4,24,8,384]{3,2,1,0:T(8,128)} %copy-done.2, f32[4,24,8,384]{3,2,1,0:T(8,128)} %copy-done.3), custom_call_target="tpu_custom_call" | custom-call | tf_op jit(solution)/shard_map/solve/pallas_call | solution.py:597
  185.3 0.0 copy-start.4
  185.3 1.0 copy-done.4
  186.3 0.0 copy-start.5
  186.3 1.0 copy-done.5
  187.3 5.3 %expand.1 = (f32[8,96,1536]{2,1,0:T(8,128)}, f32[8,24,384]{2,1,0:T(8,128)}) custom-call(f32[192,384]{1,0:T(8,128)S(1)} %bitcast.2, f32[192,384]{1,0:T(8,128)S(1)} %bitcast.3), custom_call_target="tpu_custom_call" | custom-call | tf_op jit(solution)/shard_map/expand/pallas_call | solution.py:124
Async XLA Ops:
  0.6 1.3 copy-start
  1.9 1.3 copy-start.1
  3.2 0.9 copy-start.6
  22.8 1.0 copy-start.2
  23.9 1.0 copy-start.3
  24.9 0.6 copy-start.7
  185.3 1.0 copy-start.4
  186.3 1.0 copy-start.5
where the time goes:
time: 193 us
  Pallas kernels  184 us (95%)
  local copies, waits for them, and re-layouts  8.05 us (4%)
    pallas_call x1, Pallas kernels, solve_call(): pl.pallas_call(functools.partial(solve_kernel, n_space, n_tm), out_shape=...  160 us
    pallas_call x1, Pallas kernels, restrict_call(): pl.pallas_call(restrict_kernel, grid=(sections, steps), in_specs=[pl.Bloc...  18.8 us
    unnamed x16, local copies, waits for them, and re-layouts  8.05 us
    pallas_call x1, Pallas kernels, expand_call(): pl.pallas_call(expand_kernel, grid=(part,), in_specs=[whole, whole], out_...  5.3 us

commit v1 on v0

v1 whole, which is shorter than its diff:
```python
import functools

import jax
import jax.numpy as jnp
from jax import lax
from jax.experimental import pallas as pl
from jax.experimental.pallas import tpu as pltpu
from jax.sharding import PartitionSpec as P

ITERS = 3
F32 = jnp.float32
BF16 = jnp.bfloat16
MESH = pl.DeviceIdType.MESH
SLOTS = 3
COARSE = 4


def adjoint_rows(src, co, low, count, emit):
    co_a, co_b, co_d = co
    cols = src.shape[-1]
    before = co_d[low - 1] * src[low - 1]
    y = src[low]
    here = co_d[low] * y
    for row in range(low, low + count):
        y_next = src[row + 1]
        after = co_d[row + 1] * y_next
        value = (
            co_a[row] * y
            + (before + after)
            + pltpu.roll(here, 1, 1)
            + pltpu.roll(co_b[row] * y, cols - 1, 1)
        )
        emit(row, value)
        before, here, y = here, after, y_next


def shift_groups(value, by):
    groups = value.shape[0]
    at = lax.broadcasted_iota(jnp.int32, value.shape, 0)
    outside = 0 if by == 1 else groups - 1
    return jnp.where(at == outside, 0.0, pltpu.roll(value, by % groups, 0))


def level_forward(src, dst, co):
    co_a, co_b, co_d = co
    rows, cols = src.shape[0], src.shape[-1]
    above = shift_groups(src[rows - 1], 1)
    here = first = src[0]
    for row in range(rows):
        below = src[row + 1] if row + 1 < rows else shift_groups(first, -1)
        dst[row] = (
            co_a[row] * here
            + co_d[row] * (above + below + pltpu.roll(here, cols - 1, 1))
            + co_b[row] * pltpu.roll(here, 1, 1)
        )
        above, here = here, below


def level_backward(src, dst, state, weight, co):
    co_a, co_b, co_d = co
    rows, cols = src.shape[0], src.shape[-1]
    above = shift_groups(co_d[rows - 1] * src[rows - 1], 1)
    y = src[0]
    here = first = co_d[0] * y
    for row in range(rows):
        y_next = src[row + 1] if row + 1 < rows else None
        below = shift_groups(first, -1) if y_next is None else co_d[row + 1] * y_next
        dst[row] = (
            co_a[row] * y
            + (above + below)
            + pltpu.roll(here, 1, 1)
            + pltpu.roll(co_b[row] * y, cols - 1, 1)
            + weight[row] * state[row]
        )
        above, here, y = here, below, y_next


def assimilate_kernel(
    n_space,
    n_tm,
    inn,
    obs,
    diff,
    cour,
    control,
    residual,
    inbuf,
    summed,
    turned,
    fields,
    counts,
    forcing,
    p_a,
    p_b,
    p_d,
    p_lam,
    p_send,
    p_recv,
    edge_src,
    edge_recv,
    halo_src,
    halo_recv,
    c_a,
    c_b,
    c_d,
    lam_0,
    lam_1,
    l_send,
    l_recv,
    f_recv,
    v_a,
    v_b,
    v_d,
    states,
    wts,
    adj_0,
    adj_1,
    resid,
    r_send,
    r_recv,
    red_src,
    red_tm,
    red_space,
    steps_ab,
    in_sems,
    loc_sems,
    w_send,
    w_recv,
    core_recv,
    edge_sems,
    halo_sems,
    f_sems,
    p_sems,
    l_sems,
    r_sems,
    red_tm_sems,
    red_space_sems,
):
    steps = forcing.shape[0]
    part, cols = forcing.shape[2:]
    rows = resid.shape[0]
    fine_rows = inbuf.shape[2]
    total = steps * n_tm
    halo = total - 1
    reach = steps - 1
    margin = reach + 1
    pad = halo + 1
    span = l_send.shape[1] // n_space
    pieces = cols // 128
    own_rows = steps * rows
    wide = 128 * COARSE
    n_z, n_x = n_space // 2, n_tm // 2
    place = lax.axis_index("space")
    section = lax.axis_index("tm")
    z, y = lax.div(place, 2), lax.rem(place, 2)
    x, core = lax.div(section, 2), lax.rem(section, 2)
    above, below = place - 1, place + 1
    has_above, has_below = place > 0, place < n_space - 1
    tm_peers = [lax.rem(section + k, n_tm) for k in range(1, n_tm)]
    space_peers = [lax.rem(place + k, n_space) for k in range(1, n_space)]
    lanes = [slice(piece * 128, (piece + 1) * 128) for piece in range(pieces)]

    def to(axis, peer):
        return {"device_id": {axis: peer}, "device_id_type": MESH}

    def remote(src, dst, send_sem, recv_sem, axis, peer):
        return pltpu.make_async_remote_copy(
            src_ref=src, dst_ref=dst, send_sem=send_sem, recv_sem=recv_sem, **to(axis, peer)
        )

    def slab(ref, index, size):
        return ref.at[:, pl.ds(pl.multiple_of(index * size, 8), size), :]

    def group_of(turn):
        d_x = lax.rem(lax.div(turn, 2) + 1, n_x)
        d_core = lax.rem(turn + 1, 2)
        return lax.rem(x + d_x, n_x) * 2 + lax.rem(core + d_core, 2)

    def block_copy(k):
        turn, t, slot = lax.div(k, steps), lax.rem(k, steps), lax.rem(k, SLOTS)
        return pltpu.make_async_copy(
            inn.at[t, pl.ds(group_of(turn) * part, part)], inbuf.at[slot], in_sems.at[slot]
        )

    own_counts = slab(counts.at[section], place, own_rows)
    local = []
    for piece in range(pieces):
        local.append(
            pltpu.make_async_copy(obs.at[:, lanes[piece]], own_counts.at[piece], loc_sems.at[piece, 0])
        )
        for k, field in enumerate((diff, cour)):
            local.append(
                pltpu.make_async_copy(
                    field.at[:, lanes[piece]], fields.at[k, piece], loc_sems.at[piece, 1 + k]
                )
            )
    for copy in local:
        copy.start()
    for k in range(SLOTS):
        block_copy(jnp.int32(k)).start()

    edge_recv[...] = jnp.zeros_like(edge_recv)
    halo_recv[...] = jnp.zeros_like(halo_recv)
    barrier = pltpu.get_barrier_semaphore()
    for peer in tm_peers:
        pl.semaphore_signal(barrier, inc=1, **to("tm", peer))
    for peer in space_peers:
        pl.semaphore_signal(barrier, inc=1, **to("space", peer))

    forcing[...] = jnp.zeros_like(forcing)
    p_lam[...] = jnp.zeros_like(p_lam)
    for ref in (p_a, p_b, p_d, c_a, c_b, c_d, lam_0, lam_1):
        ref[...] = jnp.zeros_like(ref)
    states[0] = jnp.zeros_like(states[0])

    for copy in local:
        copy.wait()

    def by_level(k, group, row, piece):
        return fields[k, piece, pl.ds(group * (part * rows) + row, part, stride=rows), :]

    for k in range(2):
        for piece in range(pieces):
            at = lanes[piece]
            for side, row in enumerate((0, rows - 1)):
                for group in range(n_tm):
                    edge_src[k, side, group, :, at] = by_level(k, group, row, piece)
            for side, first in enumerate((0, rows - halo)):
                for row in range(halo):
                    halo_src[k, side, row, :, at] = by_level(k, section, first + row, piece)

    pl.semaphore_wait(barrier, n_tm - 1 + n_space - 1)

    def pair(src, dst, sems):
        up = remote(src.at[0], dst.at[1], sems.at[0, 0], sems.at[1, 0], "space", above)
        down = remote(src.at[1], dst.at[0], sems.at[0, 1], sems.at[1, 1], "space", below)
        return [(has_above, has_below, up), (has_below, has_above, down)]

    def start(copies):
        for sends, _, copy in copies:
            pl.when(sends)(copy.start)

    def finish(copies):
        for sends, receives, copy in copies:
            pl.when(sends)(copy.wait_send)
            pl.when(receives)(copy.wait_recv)

    edge_copies = pair_copies = []
    edge_copies = pair(edge_src.at[0], edge_recv.at[0], edge_sems.at[0])
    edge_copies += pair(edge_src.at[1], edge_recv.at[1], edge_sems.at[1])
    start(edge_copies)

    w_copies = []
    y_peer = z * 2 + (1 - y)
    x_peers = [lax.rem(x + d_x, n_x) * 2 + core for d_x in range(1, n_x)]
    line = [lax.rem(z + k, n_z) for k in range(n_z)]
    near = [at * 2 + y for at in line]
    far = [at * 2 + (1 - y) for at in line]
    half = n_z // 2

    def count_send(owner, owner_place, axis, peer):
        block = slab(counts.at[owner], owner_place, own_rows)
        copy = remote(
            block, block, w_send.at[len(w_copies)], w_recv.at[owner, owner_place], axis, peer
        )
        copy.start()
        w_copies.append(copy)

    def count_wait(owner, owner_place):
        block = slab(counts.at[owner], owner_place, own_rows)
        remote(block, block, w_send.at[0], w_recv.at[owner, owner_place], "space", y_peer).wait_recv()

    def count_spread(owner, owner_place, along_y=True, along_x=True):
        if along_y:
            count_send(owner, owner_place, "space", y_peer)
        if along_x:
            for peer in x_peers:
                count_send(owner, owner_place, "tm", peer)

    for peer in near[1:]:
        count_send(section, place, "space", peer)
    count_spread(section, place)

    halo_copies = pair(halo_src.at[0], halo_recv.at[0], halo_sems.at[0])
    halo_copies += pair(halo_src.at[1], halo_recv.at[1], halo_sems.at[1])
    start(halo_copies)

    f_copies = []
    for k in range(2):
        for j, peer in enumerate(space_peers):
            copy = remote(
                slab(fields.at[k], section * part + peer, rows),
                slab(f_recv.at[k], place, rows),
                f_sems.at[k, 0, j],
                f_sems.at[k, 1, place],
                "space",
                peer,
            )
            copy.start()
            f_copies.append(copy)
        slab(f_recv.at[k], place, rows)[...] = slab(fields.at[k], section * part + place, rows)[...]

    pick = jnp.where(
        lax.broadcasted_iota(jnp.int32, (wide, 128), 0) // COARSE
        == lax.broadcasted_iota(jnp.int32, (wide, 128), 1),
        1.0 / (COARSE * COARSE),
        0.0,
    ).astype(BF16)

    def restrict(turn, t):
        k = turn * steps + t
        block_copy(k).wait()
        slot = lax.rem(k, SLOTS)
        for piece in range(pieces):
            block = inbuf[slot, :, :, piece * wide : (piece + 1) * wide].reshape(part * fine_rows, wide)
            summed[piece] = jnp.dot(block, pick, preferred_element_type=F32)
        pl.when(k + SLOTS < total)(lambda: block_copy(k + SLOTS).start())
        for piece in range(pieces):
            first = pl.multiple_of(place * own_rows + t * rows, 8)
            scale = counts[section, piece, pl.ds(first, rows), :].astype(F32)
            for level in range(part):
                value = summed[piece, pl.ds(level * fine_rows, rows, stride=COARSE), :]
                for sub in range(1, COARSE):
                    value += summed[piece, pl.ds(level * fine_rows + sub, rows, stride=COARSE), :]
                turned[piece, pl.ds(level, rows, stride=part), :] = value * scale
            forcing[t, pl.ds(margin, rows), :, lanes[piece]] = turned[piece].reshape(rows, part, 128)

    def put(co, row, d, c, at=slice(None), inside=None):
        a = 1.0 - 4.0 * d - c
        if inside is not None:
            a = jnp.where(inside, a, 0.0)
        co[0][row, :, at] = a
        co[1][row, :, at] = d + c
        co[2][row, :, at] = d

    p_co = (p_a, p_b, p_d)
    reach_rows = rows + 2 * reach

    def carry_back(turn):
        group = group_of(turn)
        for row in range(rows):
            for piece in range(pieces):
                d, c = by_level(0, group, row, piece), by_level(1, group, row, piece)
                put(p_co, margin + row, d, c, lanes[piece])
        put(p_co, margin - 1, edge_recv[0, 0, group], edge_recv[1, 0, group], inside=has_above)
        put(p_co, margin + rows, edge_recv[0, 1, group], edge_recv[1, 1, group], inside=has_below)
        now = forcing.at[steps - 1]
        for k in range(1, steps):
            t = steps - 1 - k

            def emit(row, value, k=k, t=t):
                value = value + forcing[t, row]
                if k < steps - 1:
                    p_lam[k % 2, row] = value
                else:
                    p_send[turn, row - (margin - reach)] = value

            adjoint_rows(now, p_co, margin - reach, reach_rows, emit)
            now = p_lam.at[k % 2]

    def p_copy(turn):
        return remote(
            p_send.at[turn],
            p_recv.at[section],
            p_sems.at[0, turn],
            p_sems.at[1, section],
            "tm",
            group_of(turn),
        )

    def one_turn(turn, carry):
        def one(t, carry):
            restrict(turn, t)
            return carry

        lax.fori_loop(0, steps, one, 0)
        pl.when(turn == 0)(lambda: finish(edge_copies))
        carry_back(turn)
        pl.when(turn < n_tm - 1)(lambda: p_copy(turn).start())
        return carry

    middle = n_tm // 2
    lax.fori_loop(0, middle, one_turn, 0)
    for at in near[1:]:
        count_wait(section, at)
        count_spread(section, at)
    lax.fori_loop(middle, n_tm, one_turn, 0)
    for k in range(n_z):
        if k >= half:
            count_wait(section, far[k])
            count_spread(section, far[k], along_y=False)
        else:
            for peer in x_peers:
                count_wait(peer, near[k])
                count_spread(peer, near[k], along_x=False)

    finish(halo_copies)
    c_co = (c_a, c_b, c_d)
    for row in range(rows):
        for piece in range(pieces):
            d, c = by_level(0, section, row, piece), by_level(1, section, row, piece)
            put(c_co, pad + row, d, c, lanes[piece])
    for row in range(halo):
        put(c_co, pad - halo + row, halo_recv[0, 0, row], halo_recv[1, 0, row], inside=has_above)
        put(c_co, pad + rows + row, halo_recv[0, 1, row], halo_recv[1, 1, row], inside=has_below)
    p_recv[section] = p_send[n_tm - 1]
    for k, peer in enumerate(tm_peers):
        p_copy(jnp.int32(k)).wait_send()
        remote(
            p_send.at[0], p_recv.at[peer], p_sems.at[0, 0], p_sems.at[1, peer], "tm", peer
        ).wait_recv()
    lam = [lam_0, lam_1]
    for row in range(reach_rows):
        lam_0[pad - reach + row] = p_recv[n_tm - 1, row]
    slot, grown = 0, reach
    for other in range(n_tm - 2, -1, -1):
        for k in range(steps):
            grown += 1
            last = other == 0 and k == steps - 1

            def emit(row, value, k=k, other=other, slot=slot, last=last):
                inside = row - (pad - reach)
                if k == steps - 1 and 0 <= inside < reach_rows:
                    value = value + p_recv[other, inside]
                if last:
                    for piece in range(pieces):
                        at = pl.ds(row - (pad - halo), part, stride=span)
                        l_send[piece, at, :] = value[:, lanes[piece]]
                else:
                    lam[1 - slot][row] = value

            adjoint_rows(lam[slot], c_co, pad - grown, rows + 2 * grown, emit)
            slot = 1 - slot

    l_copies = []
    for j, peer in enumerate(space_peers):
        copy = remote(
            slab(l_send, peer, span),
            slab(l_recv, place, span),
            l_sems.at[0, j],
            l_sems.at[1, place],
            "space",
            peer,
        )
        copy.start()
        l_copies.append(copy)
    slab(l_recv, place, span)[...] = slab(l_send, place, span)[...]

    for k in range(n_z):
        if k < half:
            count_wait(section, far[k])
        for peer in x_peers:
            if k >= half:
                count_wait(peer, near[k])
            count_wait(peer, far[k])
    first_copies = len(w_copies)
    mine = [lax.rem(x + d_x, n_x) * 2 + core for d_x in range(n_x)]
    theirs = [lax.rem(x + d_x, n_x) * 2 + (1 - core) for d_x in range(n_x)]
    for owner in mine:
        block = counts.at[owner]
        copy = remote(
            block, block, w_send.at[len(w_copies)], core_recv.at[owner], "tm", x * 2 + (1 - core)
        )
        copy.start()
        w_copies.append(copy)

    for k in range(2):
        for peer in space_peers:
            block = slab(f_recv.at[k], peer, rows)
            remote(block, block, f_sems.at[k, 0, 0], f_sems.at[k, 1, peer], "space", peer).wait_recv()
    v_co = (v_a, v_b, v_d)
    for row in range(rows):
        for piece in range(pieces):
            at = pl.ds(row, n_space, stride=rows)
            put(v_co, row, f_recv[0, piece, at, :], f_recv[1, piece, at, :], lanes[piece])

    def spread_counts(owner):
        def one(t, carry):
            for row in range(rows):
                for piece in range(pieces):
                    value = counts[owner, piece, pl.ds(t * rows + row, n_space, stride=own_rows), :]
                    wts[owner * steps + t, row, :, lanes[piece]] = value.astype(F32)
            return carry

        lax.fori_loop(0, steps, one, 0)

    for owner in mine:
        spread_counts(owner)
    for owner in theirs:
        block = counts.at[owner]
        remote(
            block, block, w_send.at[0], core_recv.at[owner], "tm", x * 2 + (1 - core)
        ).wait_recv()
        spread_counts(owner)

    for j, peer in enumerate(space_peers):
        block = slab(l_recv, peer, span)
        remote(block, block, l_sems.at[0, 0], l_sems.at[1, peer], "space", peer).wait_recv()

    def received(row, piece):
        return l_recv[piece, pl.ds(row, n_space, stride=span), :]

    for row in range(rows):
        for piece in range(pieces):
            value = received(halo + row, piece)
            from_below = row - (rows - halo)
            if from_below >= 0:
                value = value + shift_groups(received(from_below, piece), -1)
            if row < halo:
                value = value + shift_groups(received(halo + rows + row, piece), 1)
            resid[row, :, lanes[piece]] = value
            r_send[0, piece, pl.ds(row, n_space, stride=rows), :] = value

    def residual_copy(k, j, peer):
        return remote(
            slab(r_send.at[k], peer, rows),
            slab(r_recv.at[k], place, rows),
            r_sems.at[k, 0, j],
            r_sems.at[k, 1, place],
            "space",
            peer,
        )

    def send_residual(k):
        for j, peer in enumerate(space_peers):
            residual_copy(k, j, peer).start()
        slab(r_recv.at[k], place, rows)[...] = slab(r_send.at[k], place, rows)[...]

    def reduce_over(me, peers, axis, count, tile, src, slots, sems):
        src[...] = tile
        slots[me] = tile
        copies = [
            remote(src, slots.at[me], sems.at[0, j], sems.at[1, me], axis, peer)
            for j, peer in enumerate(peers)
        ]
        for copy in copies:
            copy.start()
        for j, peer in enumerate(peers):
            copies[j].wait_send()
            remote(src, slots.at[peer], sems.at[0, j], sems.at[1, peer], axis, peer).wait_recv()
        value = slots[0]
        for j in range(1, count):
            value = value + slots[j]
        return value

    def reduce_all(k, partials):
        at = lax.broadcasted_iota(jnp.int32, (8, 128), 0)
        tile = jnp.zeros((8, 128), F32)
        for j, partial in enumerate(partials):
            folded = partial[:, lanes[0]]
            for piece in range(1, pieces):
                folded = folded + partial[:, lanes[piece]]
            tile = jnp.where(at == j, jnp.sum(folded, axis=0, keepdims=True), tile)
        tile = reduce_over(
            section, tm_peers, "tm", n_tm, tile, red_src.at[k, 0], red_tm.at[k], red_tm_sems.at[k]
        )
        tile = reduce_over(
            place,
            space_peers,
            "space",
            n_space,
            tile,
            red_src.at[k, 1],
            red_space.at[k],
            red_space_sems.at[k],
        )
        sums = jnp.sum(tile, axis=1, keepdims=True)
        return [sums[j : j + 1] for j in range(len(partials))]

    adj = [adj_0, adj_1]

    def iterate(k, beta):
        send_residual(k)
        for row in range(rows):
            states[0, row] = resid[row] + beta * states[0, row]
        for t in range(1, total):
            level_forward(states.at[t - 1], states.at[t], v_co)
        for row in range(rows):
            adj_0[row] = wts[total - 1, row] * states[total - 1, row]
        slot = 0
        for t in range(total - 2, -1, -1):
            level_backward(adj[slot], adj[1 - slot], states.at[t], wts.at[t], v_co)
            slot = 1 - slot
        image = adj[slot]
        rr = dq = rq = qq = jnp.zeros((n_space, cols), F32)
        for row in range(rows):
            d, r = states[0, row], resid[row]
            q = d + image[row]
            image[row] = q
            rr, dq, rq, qq = rr + r * r, dq + d * q, rq + r * q, qq + q * q
        rr, dq, rq, qq = reduce_all(k, (rr, dq, rq, qq))
        alpha = rr / dq
        for row in range(rows):
            r = resid[row] - alpha * image[row]
            resid[row] = r
            for piece in range(pieces):
                r_send[k + 1, piece, pl.ds(row, n_space, stride=rows), :] = r[:, lanes[piece]]
        steps_ab[k, 0] = jnp.broadcast_to(alpha, (8, 128))
        steps_ab[k, 1] = jnp.broadcast_to(beta, (8, 128))
        return (rr - 2.0 * alpha * rq + alpha * alpha * qq) / rr

    lax.fori_loop(0, ITERS, iterate, jnp.zeros((1, 1), F32))
    send_residual(ITERS)

    factors = [None] * ITERS
    factor = None
    for k in range(ITERS - 1, -1, -1):
        alpha = steps_ab[k, 0, 0:1, :]
        factor = alpha if factor is None else alpha + steps_ab[k + 1, 1, 0:1, :] * factor
        factors[k] = factor

    def residual_arrived(k):
        for peer in space_peers:
            block = slab(r_recv.at[k], peer, rows)
            remote(block, block, r_sems.at[k, 0, 0], r_sems.at[k, 1, peer], "space", peer).wait_recv()

    for k in range(ITERS):
        residual_arrived(k)
    for piece in range(pieces):
        value = factors[0] * r_recv[0, piece]
        for k in range(1, ITERS):
            value = value + factors[k] * r_recv[k, piece]
        control[piece] = value
    residual_arrived(ITERS)
    residual[...] = r_recv[ITERS]

    for k in range(ITERS + 1):
        for j, peer in enumerate(space_peers):
            residual_copy(k, j, peer).wait_send()
    for copy in w_copies + f_copies + l_copies:
        copy.wait_send()


def assimilate_call(innovations, obs_counts, diffusion, courant, n_space, n_tm):
    steps, levels, fine_rows, fine_cols = innovations.shape
    part = levels // n_tm
    rows, cols = fine_rows // COARSE, fine_cols // COARSE
    pieces = cols // 128
    total = steps * n_tm
    halo = total - 1
    reach = steps - 1
    padded = rows + 2 * (reach + 1)
    ext = rows + 2 * (halo + 1)
    span = -(-(rows + 2 * halo) // 8) * 8
    row = (part, cols)
    n_x, n_z = n_tm // 2, n_space // 2
    sends = n_z - 1 + n_z * n_x + n_z * n_x + n_x
    dma = pltpu.SemaphoreType.DMA
    shapes = [
        pltpu.VMEM((SLOTS, part, fine_rows, fine_cols), BF16),
        pltpu.VMEM((pieces, part * fine_rows, 128), F32),
        pltpu.VMEM((pieces, part * rows, 128), F32),
        pltpu.VMEM((2, pieces, levels * rows, 128), F32),
        pltpu.VMEM((n_tm, pieces, n_space * steps * rows, 128), jnp.int32),
        pltpu.VMEM((steps, padded, *row), F32),
        pltpu.VMEM((padded, *row), F32),
        pltpu.VMEM((padded, *row), F32),
        pltpu.VMEM((padded, *row), F32),
        pltpu.VMEM((2, padded, *row), F32),
        pltpu.VMEM((n_tm, rows + 2 * reach, *row), F32),
        pltpu.VMEM((n_tm, rows + 2 * reach, *row), F32),
        pltpu.VMEM((2, 2, n_tm, *row), F32),
        pltpu.VMEM((2, 2, n_tm, *row), F32),
        pltpu.VMEM((2, 2, halo, *row), F32),
        pltpu.VMEM((2, 2, halo, *row), F32),
        pltpu.VMEM((ext, *row), F32),
        pltpu.VMEM((ext, *row), F32),
        pltpu.VMEM((ext, *row), F32),
        pltpu.VMEM((ext, *row), F32),
        pltpu.VMEM((ext, *row), F32),
        pltpu.VMEM((pieces, n_space * span, 128), F32),
        pltpu.VMEM((pieces, n_space * span, 128), F32),
        pltpu.VMEM((2, pieces, n_space * rows, 128), F32),
        pltpu.VMEM((rows, n_space, cols), F32),
        pltpu.VMEM((rows, n_space, cols), F32),
        pltpu.VMEM((rows, n_space, cols), F32),
        pltpu.VMEM((total, rows, n_space, cols), F32),
        pltpu.VMEM((total, rows, n_space, cols), F32),
        pltpu.VMEM((rows, n_space, cols), F32),
        pltpu.VMEM((rows, n_space, cols), F32),
        pltpu.VMEM((rows, n_space, cols), F32),
        pltpu.VMEM((ITERS + 1, pieces, n_space * rows, 128), F32),
        pltpu.VMEM((ITERS + 1, pieces, n_space * rows, 128), F32),
        pltpu.VMEM((ITERS, 2, 8, 128), F32),
        pltpu.VMEM((ITERS, n_tm, 8, 128), F32),
        pltpu.VMEM((ITERS, n_space, 8, 128), F32),
        pltpu.VMEM((ITERS, 2, 8, 128), F32),
        dma((SLOTS,)),
        dma((pieces, 3)),
        dma((sends,)),
        dma((n_tm, n_space)),
        dma((n_tm,)),
        dma((2, 2, 2)),
        dma((2, 2, 2)),
        dma((2, 2, n_space)),
        dma((2, n_tm)),
        dma((2, n_space)),
        dma((ITERS + 1, 2, n_space)),
        dma((ITERS, 2, n_tm)),
        dma((ITERS, 2, n_space)),
    ]
    out = jax.ShapeDtypeStruct((pieces, part * rows, 128), F32)
    return pl.pallas_call(
        functools.partial(assimilate_kernel, n_space, n_tm),
        out_shape=[out] * 2,
        in_specs=[pl.BlockSpec(memory_space=pl.ANY)] * 4,
        out_specs=[pl.BlockSpec(memory_space=pltpu.VMEM)] * 2,
        scratch_shapes=shapes,
        compiler_params=pltpu.CompilerParams(
            collective_id=0, has_side_effects=True, vmem_limit_bytes=60 * 2**20
        ),
        name="assimilate",
    )(
        innovations,
        obs_counts.reshape(steps * rows, cols),
        diffusion.reshape(levels * rows, cols),
        courant.reshape(levels * rows, cols),
    )


def expand_kernel(control, residual, increment, residual_out, repeated):
    rows = residual_out.shape[1]
    pieces = control.shape[0]
    wide = 128 * COARSE
    pick = jnp.where(
        lax.broadcasted_iota(jnp.int32, (128, wide), 1) // COARSE
        == lax.broadcasted_iota(jnp.int32, (128, wide), 0),
        1.0,
        0.0,
    ).astype(BF16)
    for piece in range(pieces):
        residual_out[0, :, piece * 128 : (piece + 1) * 128] = residual[piece]
        values = control[piece]
        for sub in range(COARSE):
            repeated[piece, pl.ds(sub, rows, stride=COARSE), :] = values
        rest = repeated[piece]
        total = None
        for _ in range(3):
            head = rest.astype(BF16)
            rest = rest - head.astype(F32)
            spread = jnp.dot(head, pick, preferred_element_type=F32)
            total = spread if total is None else total + spread
        increment[0, :, piece * wide : (piece + 1) * wide] = total


def expand_call(control, residual, part):
    pieces, count, _ = control.shape
    rows, cols = count // part, pieces * 128
    level = pl.BlockSpec((pieces, rows, 128), lambda l: (0, l, 0))
    return pl.pallas_call(
        expand_kernel,
        grid=(part,),
        in_specs=[level, level],
        out_specs=[
            pl.BlockSpec((1, rows * COARSE, cols * COARSE), lambda l: (l, 0, 0)),
            pl.BlockSpec((1, rows, cols), lambda l: (l, 0, 0)),
        ],
        out_shape=[
            jax.ShapeDtypeStruct((part, rows * COARSE, cols * COARSE), F32),
            jax.ShapeDtypeStruct((part, rows, cols), F32),
        ],
        scratch_shapes=[pltpu.VMEM((pieces, rows * COARSE, 128), F32)],
        compiler_params=pltpu.CompilerParams(vmem_limit_bytes=32 * 2**20),
        name="expand",
    )(control, residual)


def padded_2(cells, sides, width):
    for axis, dim in sides:
        count = lax.axis_size(axis)
        ends = count - 1
        head = lax.slice_in_dim(cells, 0, width, axis=dim)
        tail = lax.slice_in_dim(cells, cells.shape[dim] - width, cells.shape[dim], axis=dim)
        cells = jnp.concatenate(
            [
                lax.ppermute(tail, axis, [(i, (i + 1) % count) for i in range(ends)]),
                cells,
                lax.ppermute(head, axis, [((i + 1) % count, i) for i in range(ends)]),
            ],
            axis=dim,
        )
    return cells


def laplace_rows(padded, state_field):
    return (
        padded[:, 2:, :]
        + padded[:, :-2, :]
        + jnp.roll(state_field, 1, 2)
        + jnp.roll(state_field, -1, 2)
        - 4.0 * state_field
    )


def tangent(state_field, diffusion, courant):
    padded = padded_2(state_field, (("space", 1),), 1)
    return (
        state_field
        + diffusion * laplace_rows(padded, state_field)
        - courant * (state_field - jnp.roll(state_field, 1, 2))
    )


def adjoint(state_field, diffusion, courant):
    carried = courant * state_field
    spread = diffusion * state_field
    padded = padded_2(spread, (("space", 1),), 1)
    return state_field + laplace_rows(padded, spread) - carried + jnp.roll(carried, -1, 2)


def level_squares(residual):
    return lax.psum(jnp.sum(residual * residual), ("space", "tm"))


def level_curve(direction, hessian_image):
    return lax.psum(jnp.sum(direction * hessian_image), ("space", "tm"))


def solve_inner(rhs_field, hessian_part, norm_fn, curve_fn):
    control = jnp.zeros_like(rhs_field)
    residual = rhs_field
    direction = rhs_field
    norm_now = norm_fn(residual)
    for iter_no in range(ITERS):
        hessian_image = direction + hessian_part(direction)
        step_len = norm_now / curve_fn(direction, hessian_image)
        control = control + step_len * direction
        residual = residual - step_len * hessian_image
        if iter_no + 1 < ITERS:
            norm_next = norm_fn(residual)
            direction = residual + norm_next / norm_now * direction
            norm_now = norm_next
    return (control, residual)


def on_device(innovations, obs_counts, diffusion, courant):
    step_dev = obs_counts.shape[0]
    n_sections = lax.axis_size("tm")
    section_pos = lax.axis_index("tm")
    total_steps = step_dev * n_sections
    weights = obs_counts.astype(jnp.float32)[:, None]
    levels, fine_rows, fine_cols = (
        innovations.shape[1],
        innovations.shape[2],
        innovations.shape[3],
    )
    lev_part = levels // n_sections
    rows, cols = fine_rows // COARSE, fine_cols // COARSE
    n_space = lax.axis_size("space")
    tiled = lev_part == 8 and rows % 8 == 0 and cols % 128 == 0
    paired = n_space == lev_part and n_sections % 2 == 0
    if tiled and paired and rows >= total_steps - 1:
        solved = assimilate_call(innovations, obs_counts, diffusion, courant, n_space, n_sections)
        return tuple(expand_call(*solved, lev_part))
    blocks = innovations.reshape(step_dev, levels, fine_rows // 4, 4, fine_cols // 4, 4).astype(
        jnp.float32
    )
    forcing = weights * jnp.mean(blocks, axis=(3, 5))
    all_weights = lax.all_gather(obs_counts, "tm", axis=0, tiled=True).astype(jnp.float32)[:, None]
    all_forcing = lax.all_to_all(forcing, "tm", split_axis=1, concat_axis=0, tiled=True)
    diff_part = lax.dynamic_slice_in_dim(diffusion, section_pos * lev_part, lev_part, 0)
    cour_part = lax.dynamic_slice_in_dim(courant, section_pos * lev_part, lev_part, 0)

    def level_back(terms):
        current = terms[total_steps - 1]
        for step_no in range(total_steps - 2, -1, -1):
            current = terms[step_no] + adjoint(current, diff_part, cour_part)
        return current

    def level_hess(state_field):
        records = []
        for step_no in range(total_steps):
            records.append(all_weights[step_no] * state_field)
            if step_no + 1 < total_steps:
                state_field = tangent(state_field, diff_part, cour_part)
        return level_back(jnp.stack(records))

    control, residual = solve_inner(level_back(all_forcing), level_hess, level_squares, level_curve)
    increment = jnp.repeat(jnp.repeat(control, 4, axis=1), 4, axis=2)
    return (increment, residual)


def solution(mesh):
    placed = (
        P("tm", None, "space", None),
        P("tm", "space", None),
        P(None, "space", None),
        P(None, "space", None),
    )
    return jax.shard_map(
        on_device,
        mesh=mesh,
        in_specs=placed,
        out_specs=(P("tm", "space", None), P("tm", "space", None)),
        check_vma=False,
    )
```

time: 193 us -> 108 us (0.56)
  Pallas kernels: 184 us -> 106 us
  local copies, waits for them, and re-layouts: 8.05 us -> 1.92 us
    pallas_call x3 -> x2, Pallas kernels: 184 us -> 106 us  [the longest x1 100 us: assimilate_call(): pl.pallas_call(functools.partial(assimilate_kernel, n_space, n_tm), out_s...]
    unnamed x16 -> x4, local copies, waits for them, and re-layouts: 8.05 us -> 1.92 us
where the time goes in v1:
time: 108 us
  Pallas kernels  106 us (98%)
  local copies, waits for them, and re-layouts  1.92 us (2%)
    pallas_call x1, Pallas kernels, assimilate_call(): pl.pallas_call(functools.partial(assimilate_kernel, n_space, n_tm), out_s...  100 us
    pallas_call x1, Pallas kernels, expand_call(): pl.pallas_call(expand_kernel, grid=(part,), in_specs=[level, level], out_...  5.29 us

profile of v1, /device:TPU:0, one launch (start us, length us, event | category | flops | bytes accessed | tf_op | source)
XLA Modules:
  0.0 108.3 jit_solution(17647735321842588226)
XLA Ops:
  0.6 100.4 %assimilate.1 = (f32[3,192,128]{2,1,0:T(8,128)}, f32[3,192,128]{2,1,0:T(8,128)}) custom-call(bf16[3,32,96,1536]{3,2,1,0:T(8,128)(2,1)} %inn.1, s32[72,384]{1,0:T(8,128)} %bitcast.5, f32[768,384]{1,0:T(8,128)} %bitcast.3, f32[768,384]{1,0:T(8,128)} %bitcast.4), custom_call_target="tpu_custom_call" | custom-call | tf_op jit(solution)/shard_map/assimilate/pallas_call | solution.py:703
  101.1 0.0 copy-start
  101.1 1.0 copy-done
  102.0 0.0 copy-start.1
  102.0 1.0 copy-done.1
  103.0 5.3 %expand.1 = (f32[8,96,1536]{2,1,0:T(8,128)}, f32[8,24,384]{2,1,0:T(8,128)}) custom-call(f32[3,192,128]{2,1,0:T(8,128)S(1)} %copy-done, f32[3,192,128]{2,1,0:T(8,128)S(1)} %copy-done.1), custom_call_target="tpu_custom_call" | custom-call | tf_op jit(solution)/shard_map/expand/pallas_call | solution.py:750
Async XLA Ops:
  101.1 1.0 copy-start
  102.0 1.0 copy-start.1

commit v2 on v1

--- a/solution.py
+++ b/solution.py
@@ -116,11 +116,13 @@
     adj_0,
     adj_1,
     resid,
+    q_0,
+    d_1,
+    u_1,
     r_send,
     r_recv,
     red_src,
-    red_tm,
-    red_space,
+    red_recv,
     steps_ab,
     in_sems,
     loc_sems,
@@ -133,8 +135,7 @@
     p_sems,
     l_sems,
     r_sems,
-    red_tm_sems,
-    red_space_sems,
+    red_sems,
 ):
     steps = forcing.shape[0]
     part, cols = forcing.shape[2:]
@@ -158,6 +159,12 @@
     has_above, has_below = place > 0, place < n_space - 1
     tm_peers = [lax.rem(section + k, n_tm) for k in range(1, n_tm)]
     space_peers = [lax.rem(place + k, n_space) for k in range(1, n_space)]
+    everyone = [
+        {"space": lax.rem(place + j, n_space), "tm": lax.rem(section + k, n_tm)}
+        for j in range(n_space)
+        for k in range(n_tm)
+        if j or k
+    ]
     lanes = [slice(piece * 128, (piece + 1) * 128) for piece in range(pieces)]
 
     def to(axis, peer):
@@ -196,25 +203,23 @@
             )
     for copy in local:
         copy.start()
-    for k in range(SLOTS):
-        block_copy(jnp.int32(k)).start()
+    block_copy(jnp.int32(0)).start()
 
     edge_recv[...] = jnp.zeros_like(edge_recv)
     halo_recv[...] = jnp.zeros_like(halo_recv)
     barrier = pltpu.get_barrier_semaphore()
-    for peer in tm_peers:
-        pl.semaphore_signal(barrier, inc=1, **to("tm", peer))
-    for peer in space_peers:
-        pl.semaphore_signal(barrier, inc=1, **to("space", peer))
+    for peer in everyone:
+        pl.semaphore_signal(barrier, inc=1, device_id=peer, device_id_type=MESH)
 
     forcing[...] = jnp.zeros_like(forcing)
     p_lam[...] = jnp.zeros_like(p_lam)
     for ref in (p_a, p_b, p_d, c_a, c_b, c_d, lam_0, lam_1):
         ref[...] = jnp.zeros_like(ref)
-    states[0] = jnp.zeros_like(states[0])
 
     for copy in local:
         copy.wait()
+    for k in range(1, SLOTS):
+        block_copy(jnp.int32(k)).start()
 
     def by_level(k, group, row, piece):
         return fields[k, piece, pl.ds(group * (part * rows) + row, part, stride=rows), :]
@@ -229,7 +234,7 @@
                 for row in range(halo):
                     halo_src[k, side, row, :, at] = by_level(k, section, first + row, piece)
 
-    pl.semaphore_wait(barrier, n_tm - 1 + n_space - 1)
+    pl.semaphore_wait(barrier, len(everyone))
 
     def pair(src, dst, sems):
         up = remote(src.at[0], dst.at[1], sems.at[0, 0], sems.at[1, 0], "space", above)
@@ -250,55 +255,75 @@
     edge_copies += pair(edge_src.at[1], edge_recv.at[1], edge_sems.at[1])
     start(edge_copies)
 
+    halo_copies = pair(halo_src.at[0], halo_recv.at[0], halo_sems.at[0])
+    halo_copies += pair(halo_src.at[1], halo_recv.at[1], halo_sems.at[1])
+
     w_copies = []
+    x_peers = [lax.rem(x + d_x, n_x) * 2 + core for d_x in range(1, n_x)]
     y_peer = z * 2 + (1 - y)
-    x_peers = [lax.rem(x + d_x, n_x) * 2 + core for d_x in range(1, n_x)]
-    line = [lax.rem(z + k, n_z) for k in range(n_z)]
-    near = [at * 2 + y for at in line]
-    far = [at * 2 + (1 - y) for at in line]
-    half = n_z // 2
-
-    def count_send(owner, owner_place, axis, peer):
-        block = slab(counts.at[owner], owner_place, own_rows)
+
+    def count_block(owner, owner_place):
+        return slab(counts.at[owner], owner_place, own_rows)
+
+    def count_send(owner, owner_place, axis, peer, valid=None):
+        block = count_block(owner, owner_place)
         copy = remote(
             block, block, w_send.at[len(w_copies)], w_recv.at[owner, owner_place], axis, peer
         )
-        copy.start()
-        w_copies.append(copy)
-
-    def count_wait(owner, owner_place):
-        block = slab(counts.at[owner], owner_place, own_rows)
-        remote(block, block, w_send.at[0], w_recv.at[owner, owner_place], "space", y_peer).wait_recv()
-
-    def count_spread(owner, owner_place, along_y=True, along_x=True):
-        if along_y:
-            count_send(owner, owner_place, "space", y_peer)
-        if along_x:
+        if valid is None:
+            copy.start()
+        else:
+            pl.when(valid)(copy.start)
+        w_copies.append((valid, copy))
+
+    def count_wait(owner, owner_place, valid=None):
+        block = count_block(owner, owner_place)
+        copy = remote(block, block, w_send.at[0], w_recv.at[owner, owner_place], "space", y_peer)
+        if valid is None:
+            copy.wait_recv()
+        else:
+            pl.when(valid)(copy.wait_recv)
+
+    def inside_line(at):
+        return jnp.logical_and(at >= 0, at < n_z)
+
+    def count_pass(distance):
+        for sign in (-1, 1) if distance else (0,):
+            at = z + sign * distance
+            valid = inside_line(at) if distance else None
+            owner_place = at * 2 + y
+            if distance:
+                count_wait(section, owner_place, valid)
+            for onward in (-sign,) if distance else (-1, 1):
+                goes = inside_line(z + onward)
+                if distance:
+                    goes = jnp.logical_and(valid, goes)
+                if distance < n_z - 1:
+                    count_send(section, owner_place, "space", place + 2 * onward, goes)
+            count_send(section, owner_place, "space", y_peer, valid)
             for peer in x_peers:
-                count_send(owner, owner_place, "tm", peer)
-
-    for peer in near[1:]:
-        count_send(section, place, "space", peer)
-    count_spread(section, place)
-
-    halo_copies = pair(halo_src.at[0], halo_recv.at[0], halo_sems.at[0])
-    halo_copies += pair(halo_src.at[1], halo_recv.at[1], halo_sems.at[1])
-    start(halo_copies)
+                count_send(section, owner_place, "tm", peer, valid)
+
+    count_pass(0)
 
     f_copies = []
-    for k in range(2):
-        for j, peer in enumerate(space_peers):
-            copy = remote(
-                slab(fields.at[k], section * part + peer, rows),
-                slab(f_recv.at[k], place, rows),
-                f_sems.at[k, 0, j],
-                f_sems.at[k, 1, place],
-                "space",
-                peer,
-            )
-            copy.start()
-            f_copies.append(copy)
-        slab(f_recv.at[k], place, rows)[...] = slab(fields.at[k], section * part + place, rows)[...]
+
+    def send_fields():
+        for k in range(2):
+            for j, peer in enumerate(space_peers):
+                copy = remote(
+                    slab(fields.at[k], section * part + peer, rows),
+                    slab(f_recv.at[k], place, rows),
+                    f_sems.at[k, 0, j],
+                    f_sems.at[k, 1, place],
+                    "space",
+                    peer,
+                )
+                copy.start()
+                f_copies.append(copy)
+            slab(f_recv.at[k], place, rows)[...] = slab(
+                fields.at[k], section * part + place, rows
+            )[...]
 
     pick = jnp.where(
         lax.broadcasted_iota(jnp.int32, (wide, 128), 0) // COARSE
@@ -368,31 +393,23 @@
             group_of(turn),
         )
 
-    def one_turn(turn, carry):
-        def one(t, carry):
-            restrict(turn, t)
-            return carry
-
-        lax.fori_loop(0, steps, one, 0)
-        pl.when(turn == 0)(lambda: finish(edge_copies))
-        carry_back(turn)
-        pl.when(turn < n_tm - 1)(lambda: p_copy(turn).start())
-        return carry
-
-    middle = n_tm // 2
-    lax.fori_loop(0, middle, one_turn, 0)
-    for at in near[1:]:
-        count_wait(section, at)
-        count_spread(section, at)
-    lax.fori_loop(middle, n_tm, one_turn, 0)
-    for k in range(n_z):
-        if k >= half:
-            count_wait(section, far[k])
-            count_spread(section, far[k], along_y=False)
-        else:
-            for peer in x_peers:
-                count_wait(peer, near[k])
-                count_spread(peer, near[k], along_x=False)
+    def one_step(t, turn):
+        restrict(turn, t)
+        return turn
+
+    for turn in range(n_tm):
+        lax.fori_loop(0, steps, one_step, jnp.int32(turn))
+        if turn == 0:
+            finish(edge_copies)
+            start(halo_copies)
+        carry_back(jnp.int32(turn))
+        if turn < n_tm - 1:
+            p_copy(jnp.int32(turn)).start()
+        for distance in range(1, n_z):
+            if distance % n_tm == turn + 1:
+                count_pass(distance)
+        if turn == 1:
+            send_fields()
 
     finish(halo_copies)
     c_co = (c_a, c_b, c_d)
@@ -446,24 +463,12 @@
         l_copies.append(copy)
     slab(l_recv, place, span)[...] = slab(l_send, place, span)[...]
 
-    for k in range(n_z):
-        if k < half:
-            count_wait(section, far[k])
+    line = [lax.rem(z + k, n_z) for k in range(n_z)]
+    for at in line:
+        owner_place = at * 2 + (1 - y)
+        count_wait(section, owner_place)
         for peer in x_peers:
-            if k >= half:
-                count_wait(peer, near[k])
-            count_wait(peer, far[k])
-    first_copies = len(w_copies)
-    mine = [lax.rem(x + d_x, n_x) * 2 + core for d_x in range(n_x)]
-    theirs = [lax.rem(x + d_x, n_x) * 2 + (1 - core) for d_x in range(n_x)]
-    for owner in mine:
-        block = counts.at[owner]
-        copy = remote(
-            block, block, w_send.at[len(w_copies)], core_recv.at[owner], "tm", x * 2 + (1 - core)
-        )
-        copy.start()
-        w_copies.append(copy)
-
+            count_send(section, owner_place, "tm", peer)
     for k in range(2):
         for peer in space_peers:
             block = slab(f_recv.at[k], peer, rows)
@@ -473,6 +478,20 @@
         for piece in range(pieces):
             at = pl.ds(row, n_space, stride=rows)
             put(v_co, row, f_recv[0, piece, at, :], f_recv[1, piece, at, :], lanes[piece])
+
+    for at in line:
+        for peer in x_peers:
+            count_wait(peer, at * 2 + y)
+            count_wait(peer, at * 2 + (1 - y))
+    mine = [lax.rem(x + d_x, n_x) * 2 + core for d_x in range(n_x)]
+    theirs = [lax.rem(x + d_x, n_x) * 2 + (1 - core) for d_x in range(n_x)]
+    for owner in mine:
+        block = counts.at[owner]
+        copy = remote(
+            block, block, w_send.at[len(w_copies)], core_recv.at[owner], "tm", x * 2 + (1 - core)
+        )
+        copy.start()
+        w_copies.append((None, copy))
 
     def spread_counts(owner):
         def one(t, carry):
@@ -526,53 +545,140 @@
             residual_copy(k, j, peer).start()
         slab(r_recv.at[k], place, rows)[...] = slab(r_send.at[k], place, rows)[...]
 
-    def reduce_over(me, peers, axis, count, tile, src, slots, sems):
-        src[...] = tile
-        slots[me] = tile
-        copies = [
-            remote(src, slots.at[me], sems.at[0, j], sems.at[1, me], axis, peer)
-            for j, peer in enumerate(peers)
-        ]
-        for copy in copies:
-            copy.start()
-        for j, peer in enumerate(peers):
-            copies[j].wait_send()
-            remote(src, slots.at[peer], sems.at[0, j], sems.at[1, peer], axis, peer).wait_recv()
-        value = slots[0]
-        for j in range(1, count):
-            value = value + slots[j]
-        return value
-
-    def reduce_all(k, partials):
-        at = lax.broadcasted_iota(jnp.int32, (8, 128), 0)
-        tile = jnp.zeros((8, 128), F32)
+    def peer_slot(peer):
+        return peer["tm"] * n_space + peer["space"]
+
+    me = section * n_space + place
+
+    def reduce_all(k, partials, meanwhile):
+        at = lax.broadcasted_iota(jnp.int32, (16, 128), 0)
+        lane = lax.broadcasted_iota(jnp.int32, (16, 128), 1)
+        tile = jnp.zeros((16, 128), F32)
         for j, partial in enumerate(partials):
             folded = partial[:, lanes[0]]
             for piece in range(1, pieces):
                 folded = folded + partial[:, lanes[piece]]
             tile = jnp.where(at == j, jnp.sum(folded, axis=0, keepdims=True), tile)
-        tile = reduce_over(
-            section, tm_peers, "tm", n_tm, tile, red_src.at[k, 0], red_tm.at[k], red_tm_sems.at[k]
-        )
-        tile = reduce_over(
-            place,
-            space_peers,
-            "space",
-            n_space,
-            tile,
-            red_src.at[k, 1],
-            red_space.at[k],
-            red_space_sems.at[k],
-        )
-        sums = jnp.sum(tile, axis=1, keepdims=True)
-        return [sums[j : j + 1] for j in range(len(partials))]
+        tile = jnp.where(at == lane, jnp.sum(tile, axis=1, keepdims=True), 0.0)
+        line = jnp.sum(tile, axis=0, keepdims=True)
+        red_src[k] = line
+        red_recv[k, me] = line
+        copies = [
+            pltpu.make_async_remote_copy(
+                src_ref=red_src.at[k],
+                dst_ref=red_recv.at[k, me],
+                send_sem=red_sems.at[k, 0, j],
+                recv_sem=red_sems.at[k, 1, me],
+                device_id=peer,
+                device_id_type=MESH,
+            )
+            for j, peer in enumerate(everyone)
+        ]
+        for copy in copies:
+            copy.start()
+        meanwhile()
+        for j, peer in enumerate(everyone):
+            copies[j].wait_send()
+            pltpu.make_async_remote_copy(
+                src_ref=red_src.at[k],
+                dst_ref=red_recv.at[k, peer_slot(peer)],
+                send_sem=red_sems.at[k, 0, j],
+                recv_sem=red_sems.at[k, 1, peer_slot(peer)],
+                device_id=peer,
+                device_id_type=MESH,
+            ).wait_recv()
+        line = red_recv[k, 0]
+        for j in range(1, n_tm * n_space):
+            line = line + red_recv[k, j]
+        line = jnp.broadcast_to(line, (8, 128))
+        lane = lane[:8]
+        return [
+            jnp.sum(jnp.where(lane == j, line, 0.0), axis=1, keepdims=True)[0:1]
+            for j in range(len(partials))
+        ]
 
     adj = [adj_0, adj_1]
-
-    def iterate(k, beta):
-        send_residual(k)
+    image = adj[(total - 1) % 2]
+
+    def keep_residual(k, row, value):
+        for piece in range(pieces):
+            r_send[k, piece, pl.ds(row, n_space, stride=rows), :] = value[:, lanes[piece]]
+
+    def scalar(k):
+        return steps_ab[k, 0:1, 0:1]
+
+    def set_scalar(k, value):
+        steps_ab[k] = jnp.broadcast_to(value, (8, 128))
+
+    def dots(names, vectors):
+        sums = [jnp.zeros((n_space, cols), F32)] * len(names)
         for row in range(rows):
-            states[0, row] = resid[row] + beta * states[0, row]
+            at = vectors(row)
+            sums = [total_ + at[pair_[0]] * at[pair_[1]] for total_, pair_ in zip(sums, names)]
+        return sums
+
+    def first_step():
+        def vectors(row):
+            r = resid[row]
+            q = r + image[row]
+            q_0[row] = q
+            return {"r": r, "q": q}
+
+        rr, rq, qq = reduce_all(0, dots(("rr", "rq", "qq"), vectors), lambda: send_residual(0))
+        alpha = rr / rq
+        beta = (rr - 2.0 * alpha * rq + alpha * alpha * qq) / rr
+        set_scalar(0, alpha)
+        set_scalar(1, beta)
+        for row in range(rows):
+            r_0 = resid[row]
+            r = r_0 - alpha * q_0[row]
+            resid[row] = r
+            keep_residual(1, row, r)
+            d = r + beta * r_0
+            d_1[row] = d
+            states[0, row] = d
+        send_residual(1)
+
+    def second_image():
+        for row in range(rows):
+            u = states[0, row] + image[row]
+            u_1[row] = u
+            states[0, row] = u
+            keep_residual(2, row, u)
+
+    def last_steps():
+        def vectors(row):
+            u = u_1[row]
+            v = u + image[row]
+            image[row] = v
+            return {"r": resid[row], "d": d_1[row], "u": u, "v": v, "q": q_0[row]}
+
+        names = ("rr", "du", "ru", "uu", "rq", "uq", "dq", "rv", "uv", "dv")
+        rr, du, ru, uu, rq, uq, dq, rv, uv, dv = reduce_all(
+            1, dots(names, vectors), lambda: send_residual(2)
+        )
+        beta_1 = scalar(1)
+        alpha = rr / du
+        rr_2 = rr - 2.0 * alpha * ru + alpha * alpha * uu
+        beta = rr_2 / rr
+        on_u, on_q, on_v = 1.0 + beta, -beta_1, -alpha
+        curve = (
+            (on_u * ru + on_q * rq + on_v * rv)
+            - alpha * (on_u * uu + on_q * uq + on_v * uv)
+            + beta * (on_u * du + on_q * dq + on_v * dv)
+        )
+        alpha_2 = rr_2 / curve
+        for row in range(rows):
+            u = u_1[row]
+            r_2 = resid[row] - alpha * u
+            keep_residual(3, row, r_2 - alpha_2 * (on_u * u + on_q * q_0[row] + on_v * image[row]))
+        send_residual(3)
+        kept = alpha + alpha_2 * beta
+        set_scalar(2, scalar(0) + kept * beta_1)
+        set_scalar(3, kept + alpha_2)
+        set_scalar(4, -alpha * alpha_2)
+
+    def one_product(k, carry):
         for t in range(1, total):
             level_forward(states.at[t - 1], states.at[t], v_co)
         for row in range(rows):
@@ -581,33 +687,13 @@
         for t in range(total - 2, -1, -1):
             level_backward(adj[slot], adj[1 - slot], states.at[t], wts.at[t], v_co)
             slot = 1 - slot
-        image = adj[slot]
-        rr = dq = rq = qq = jnp.zeros((n_space, cols), F32)
-        for row in range(rows):
-            d, r = states[0, row], resid[row]
-            q = d + image[row]
-            image[row] = q
-            rr, dq, rq, qq = rr + r * r, dq + d * q, rq + r * q, qq + q * q
-        rr, dq, rq, qq = reduce_all(k, (rr, dq, rq, qq))
-        alpha = rr / dq
-        for row in range(rows):
-            r = resid[row] - alpha * image[row]
-            resid[row] = r
-            for piece in range(pieces):
-                r_send[k + 1, piece, pl.ds(row, n_space, stride=rows), :] = r[:, lanes[piece]]
-        steps_ab[k, 0] = jnp.broadcast_to(alpha, (8, 128))
-        steps_ab[k, 1] = jnp.broadcast_to(beta, (8, 128))
-        return (rr - 2.0 * alpha * rq + alpha * alpha * qq) / rr
-
-    lax.fori_loop(0, ITERS, iterate, jnp.zeros((1, 1), F32))
-    send_residual(ITERS)
-
-    factors = [None] * ITERS
-    factor = None
-    for k in range(ITERS - 1, -1, -1):
-        alpha = steps_ab[k, 0, 0:1, :]
-        factor = alpha if factor is None else alpha + steps_ab[k + 1, 1, 0:1, :] * factor
-        factors[k] = factor
+        pl.when(k == 0)(first_step)
+        pl.when(k == 1)(second_image)
+        pl.when(k == 2)(last_steps)
+        return carry
+
+    states[0] = resid[...]
+    lax.fori_loop(0, ITERS, one_product, 0)
 
     def residual_arrived(k):
         for peer in space_peers:
@@ -617,9 +703,9 @@
     for k in range(ITERS):
         residual_arrived(k)
     for piece in range(pieces):
-        value = factors[0] * r_recv[0, piece]
+        value = steps_ab[2, 0:1, :] * r_recv[0, piece]
         for k in range(1, ITERS):
-            value = value + factors[k] * r_recv[k, piece]
+            value = value + steps_ab[2 + k, 0:1, :] * r_recv[k, piece]
         control[piece] = value
     residual_arrived(ITERS)
     residual[...] = r_recv[ITERS]
@@ -627,7 +713,12 @@
     for k in range(ITERS + 1):
         for j, peer in enumerate(space_peers):
             residual_copy(k, j, peer).wait_send()
-    for copy in w_copies + f_copies + l_copies:
+    for valid, copy in w_copies:
+        if valid is None:
+            copy.wait_send()
+        else:
+            pl.when(valid)(copy.wait_send)
+    for copy in f_copies + l_copies:
         copy.wait_send()
 
 
@@ -644,7 +735,7 @@
     span = -(-(rows + 2 * halo) // 8) * 8
     row = (part, cols)
     n_x, n_z = n_tm // 2, n_space // 2
-    sends = n_z - 1 + n_z * n_x + n_z * n_x + n_x
+    sends = 2 + n_x + 2 * (n_z - 1) * (1 + n_x) + n_z * (n_x - 1) + n_x
     dma = pltpu.SemaphoreType.DMA
     shapes = [
         pltpu.VMEM((SLOTS, part, fine_rows, fine_cols), BF16),
@@ -679,12 +770,14 @@
         pltpu.VMEM((rows, n_space, cols), F32),
         pltpu.VMEM((rows, n_space, cols), F32),
         pltpu.VMEM((rows, n_space, cols), F32),
+        pltpu.VMEM((rows, n_space, cols), F32),
+        pltpu.VMEM((rows, n_space, cols), F32),
+        pltpu.VMEM((rows, n_space, cols), F32),
         pltpu.VMEM((ITERS + 1, pieces, n_space * rows, 128), F32),
         pltpu.VMEM((ITERS + 1, pieces, n_space * rows, 128), F32),
-        pltpu.VMEM((ITERS, 2, 8, 128), F32),
-        pltpu.VMEM((ITERS, n_tm, 8, 128), F32),
-        pltpu.VMEM((ITERS, n_space, 8, 128), F32),
-        pltpu.VMEM((ITERS, 2, 8, 128), F32),
+        pltpu.VMEM((2, 1, 128), F32),
+        pltpu.VMEM((2, n_tm * n_space, 1, 128), F32),
+        pltpu.VMEM((5, 8, 128), F32),
         dma((SLOTS,)),
         dma((pieces, 3)),
         dma((sends,)),
@@ -696,8 +789,7 @@
         dma((2, n_tm)),
         dma((2, n_space)),
         dma((ITERS + 1, 2, n_space)),
-        dma((ITERS, 2, n_tm)),
-        dma((ITERS, 2, n_space)),
+        dma((2, 2, n_tm * n_space)),
     ]
     out = jax.ShapeDtypeStruct((pieces, part * rows, 128), F32)
     return pl.pallas_call(
@@ -718,51 +810,76 @@
     )
 
 
-def expand_kernel(control, residual, increment, residual_out, repeated):
-    rows = residual_out.shape[1]
-    pieces = control.shape[0]
+def expand_kernel(control, residual, increment, residual_out, held, passed, repeated, wide_out, in_sems, out_sems):
+    pieces, part, rows, _ = control.shape
     wide = 128 * COARSE
+    arrive = []
+    for k, (src, dst) in enumerate(((control, held), (residual, passed))):
+        arrive.append(pltpu.make_async_copy(src, dst, in_sems.at[k]))
+        arrive[k].start()
     pick = jnp.where(
-        lax.broadcasted_iota(jnp.int32, (128, wide), 1) // COARSE
-        == lax.broadcasted_iota(jnp.int32, (128, wide), 0),
+        lax.broadcasted_iota(jnp.int32, (256, wide), 1) // COARSE
+        == lax.rem(lax.broadcasted_iota(jnp.int32, (256, wide), 0), 128),
         1.0,
         0.0,
     ).astype(BF16)
-    for piece in range(pieces):
-        residual_out[0, :, piece * 128 : (piece + 1) * 128] = residual[piece]
-        values = control[piece]
-        for sub in range(COARSE):
-            repeated[piece, pl.ds(sub, rows, stride=COARSE), :] = values
-        rest = repeated[piece]
-        total = None
-        for _ in range(3):
-            head = rest.astype(BF16)
-            rest = rest - head.astype(F32)
-            spread = jnp.dot(head, pick, preferred_element_type=F32)
-            total = spread if total is None else total + spread
-        increment[0, :, piece * wide : (piece + 1) * wide] = total
+    leave = []
+    arrive[0].wait()
+    for level in range(part):
+        for piece in range(pieces):
+            values = held[piece, level]
+            for sub in range(COARSE):
+                repeated[level % 2, piece, pl.ds(sub, rows, stride=COARSE), :] = values
+            whole = repeated[level % 2, piece]
+            head = whole.astype(BF16)
+            rest = (whole - head.astype(F32)).astype(BF16)
+            both = jnp.concatenate([head, rest], axis=1)
+            wide_out[level, :, piece * wide : (piece + 1) * wide] = jnp.dot(
+                both, pick, preferred_element_type=F32
+            )
+        leave.append(
+            pltpu.make_async_copy(wide_out.at[level], increment.at[level], out_sems.at[level])
+        )
+        leave[-1].start()
+        if level == 0:
+            arrive[1].wait()
+            for piece in range(pieces):
+                at = pl.ds(piece * 128, 128)
+                leave.append(
+                    pltpu.make_async_copy(
+                        passed.at[piece], residual_out.at[:, :, at], out_sems.at[part + piece]
+                    )
+                )
+                leave[-1].start()
+    for copy in leave:
+        copy.wait()
 
 
 def expand_call(control, residual, part):
     pieces, count, _ = control.shape
     rows, cols = count // part, pieces * 128
-    level = pl.BlockSpec((pieces, rows, 128), lambda l: (0, l, 0))
+    fine = (part, rows * COARSE, cols * COARSE)
+    cut = (pieces, part, rows, 128)
+    dma = pltpu.SemaphoreType.DMA
     return pl.pallas_call(
         expand_kernel,
-        grid=(part,),
-        in_specs=[level, level],
-        out_specs=[
-            pl.BlockSpec((1, rows * COARSE, cols * COARSE), lambda l: (l, 0, 0)),
-            pl.BlockSpec((1, rows, cols), lambda l: (l, 0, 0)),
-        ],
+        in_specs=[pl.BlockSpec(memory_space=pl.ANY)] * 2,
+        out_specs=[pl.BlockSpec(memory_space=pl.ANY)] * 2,
         out_shape=[
-            jax.ShapeDtypeStruct((part, rows * COARSE, cols * COARSE), F32),
+            jax.ShapeDtypeStruct(fine, F32),
             jax.ShapeDtypeStruct((part, rows, cols), F32),
         ],
-        scratch_shapes=[pltpu.VMEM((pieces, rows * COARSE, 128), F32)],
-        compiler_params=pltpu.CompilerParams(vmem_limit_bytes=32 * 2**20),
+        scratch_shapes=[
+            pltpu.VMEM(cut, F32),
+            pltpu.VMEM(cut, F32),
+            pltpu.VMEM((2, pieces, rows * COARSE, 128), F32),
+            pltpu.VMEM(fine, F32),
+            dma((2,)),
+            dma((part + pieces,)),
+        ],
+        compiler_params=pltpu.CompilerParams(vmem_limit_bytes=67_043_328),
         name="expand",
-    )(control, residual)
+    )(control.reshape(cut), residual.reshape(cut))
 
 
 def padded_2(cells, sides, width):

time: 108 us -> 89.9 us (0.83)
  Pallas kernels: 106 us -> 88.9 us
  local copies, waits for them, and re-layouts: 1.92 us -> 0 us
    pallas_call x1, Pallas kernels: 100 us -> 85.3 us  [assimilate_call(): pl.pallas_call(functools.partial(assimilate_kernel, n_space, n_tm), out_s...]
    unnamed x4 -> x0, local copies, waits for them, and re-layouts: 1.92 us -> none
    pallas_call x1, Pallas kernels: 5.29 us -> 3.6 us  [expand_call(): pl.pallas_call(expand_kernel, in_specs=[pl.BlockSpec(memory_space=pl.ANY)...]
where the time goes in v2:
time: 89.9 us; the launch traced here: 89.7 us
  Pallas kernels  88.9 us (99%)
    pallas_call x1, Pallas kernels, assimilate_call(): pl.pallas_call(functools.partial(assimilate_kernel, n_space, n_tm), out_s...  85.3 us
    pallas_call x1, Pallas kernels, expand_call(): pl.pallas_call(expand_kernel, in_specs=[pl.BlockSpec(memory_space=pl.ANY)...  3.6 us

profile of v2, /device:TPU:0, one launch (start us, length us, event | category | flops | bytes accessed | tf_op | source)
XLA Modules:
  0.0 89.7 jit_solution(6016232195705173188)
XLA Ops:
  0.6 85.3 %assimilate.1 = (f32[3,192,128]{2,1,0:T(8,128)}, f32[3,192,128]{2,1,0:T(8,128)}) custom-call(bf16[3,32,96,1536]{3,2,1,0:T(8,128)(2,1)} %inn.1, s32[72,384]{1,0:T(8,128)} %bitcast.9, f32[768,384]{1,0:T(8,128)} %bitcast.5, f32[768,384]{1,0:T(8,128)} %bitcast.6), custom_call_target="tpu_custom_call" | custom-call | tf_op jit(solution)/shard_map/assimilate/pallas_call | solution.py:795
  86.0 3.6 %expand.1 = (f32[8,96,1536]{2,1,0:T(8,128)}, f32[8,24,384]{2,1,0:T(8,128)}) custom-call(f32[3,8,24,128]{3,2,1,0:T(8,128)} %bitcast.7, f32[3,8,24,128]{3,2,1,0:T(8,128)} %bitcast.8), custom_call_target="tpu_custom_call" | custom-call | tf_op jit(solution)/shard_map/expand/pallas_call | solution.py:864

commit v3 on v2

--- a/solution.py
+++ b/solution.py
@@ -143,6 +143,7 @@
     fine_rows = inbuf.shape[2]
     total = steps * n_tm
     halo = total - 1
+    apron = halo - 1
     reach = steps - 1
     margin = reach + 1
     pad = halo + 1
@@ -230,8 +231,8 @@
             for side, row in enumerate((0, rows - 1)):
                 for group in range(n_tm):
                     edge_src[k, side, group, :, at] = by_level(k, group, row, piece)
-            for side, first in enumerate((0, rows - halo)):
-                for row in range(halo):
+            for side, first in enumerate((0, rows - apron)):
+                for row in range(apron):
                     halo_src[k, side, row, :, at] = by_level(k, section, first + row, piece)
 
     pl.semaphore_wait(barrier, len(everyone))
@@ -406,7 +407,7 @@
         if turn < n_tm - 1:
             p_copy(jnp.int32(turn)).start()
         for distance in range(1, n_z):
-            if distance % n_tm == turn + 1:
+            if distance % n_tm == turn:
                 count_pass(distance)
         if turn == 1:
             send_fields()
@@ -417,8 +418,8 @@
         for piece in range(pieces):
             d, c = by_level(0, section, row, piece), by_level(1, section, row, piece)
             put(c_co, pad + row, d, c, lanes[piece])
-    for row in range(halo):
-        put(c_co, pad - halo + row, halo_recv[0, 0, row], halo_recv[1, 0, row], inside=has_above)
+    for row in range(apron):
+        put(c_co, pad - apron + row, halo_recv[0, 0, row], halo_recv[1, 0, row], inside=has_above)
         put(c_co, pad + rows + row, halo_recv[0, 1, row], halo_recv[1, 1, row], inside=has_below)
     p_recv[section] = p_send[n_tm - 1]
     for k, peer in enumerate(tm_peers):
@@ -469,6 +470,17 @@
         count_wait(section, owner_place)
         for peer in x_peers:
             count_send(section, owner_place, "tm", peer)
+    core_peer = x * 2 + (1 - core)
+
+    def core_send(owner):
+        block = counts.at[owner]
+        copy = remote(
+            block, block, w_send.at[len(w_copies)], core_recv.at[owner], "tm", core_peer
+        )
+        copy.start()
+        w_copies.append((None, copy))
+
+    core_send(section)
     for k in range(2):
         for peer in space_peers:
             block = slab(f_recv.at[k], peer, rows)
@@ -483,15 +495,8 @@
         for peer in x_peers:
             count_wait(peer, at * 2 + y)
             count_wait(peer, at * 2 + (1 - y))
-    mine = [lax.rem(x + d_x, n_x) * 2 + core for d_x in range(n_x)]
-    theirs = [lax.rem(x + d_x, n_x) * 2 + (1 - core) for d_x in range(n_x)]
-    for owner in mine:
-        block = counts.at[owner]
-        copy = remote(
-            block, block, w_send.at[len(w_copies)], core_recv.at[owner], "tm", x * 2 + (1 - core)
-        )
-        copy.start()
-        w_copies.append((None, copy))
+    for owner in x_peers:
+        core_send(owner)
 
     def spread_counts(owner):
         def one(t, carry):
@@ -502,15 +507,6 @@
             return carry
 
         lax.fori_loop(0, steps, one, 0)
-
-    for owner in mine:
-        spread_counts(owner)
-    for owner in theirs:
-        block = counts.at[owner]
-        remote(
-            block, block, w_send.at[0], core_recv.at[owner], "tm", x * 2 + (1 - core)
-        ).wait_recv()
-        spread_counts(owner)
 
     for j, peer in enumerate(space_peers):
         block = slab(l_recv, peer, span)
@@ -540,9 +536,11 @@
             peer,
         )
 
-    def send_residual(k):
-        for j, peer in enumerate(space_peers):
+    def send_residual(k, first=0, last=n_space - 1):
+        for j, peer in list(enumerate(space_peers))[first:last]:
             residual_copy(k, j, peer).start()
+        if first:
+            return
         slab(r_recv.at[k], place, rows)[...] = slab(r_send.at[k], place, rows)[...]
 
     def peer_slot(peer):
@@ -617,14 +615,28 @@
             sums = [total_ + at[pair_[0]] * at[pair_[1]] for total_, pair_ in zip(sums, names)]
         return sums
 
+    def take_counts():
+        for owner in (section, *x_peers):
+            spread_counts(owner)
+        for d_x in range(n_x):
+            owner = lax.rem(x + d_x, n_x) * 2 + (1 - core)
+            block = counts.at[owner]
+            remote(block, block, w_send.at[0], core_recv.at[owner], "tm", core_peer).wait_recv()
+            spread_counts(owner)
+
+    def send_first():
+        send_residual(0)
+        send_residual(1)
+
     def first_step():
         def vectors(row):
             r = resid[row]
             q = r + image[row]
             q_0[row] = q
+            keep_residual(1, row, q)
             return {"r": r, "q": q}
 
-        rr, rq, qq = reduce_all(0, dots(("rr", "rq", "qq"), vectors), lambda: send_residual(0))
+        rr, rq, qq = reduce_all(0, dots(("rr", "rq", "qq"), vectors), send_first)
         alpha = rr / rq
         beta = (rr - 2.0 * alpha * rq + alpha * alpha * qq) / rr
         set_scalar(0, alpha)
@@ -633,11 +645,9 @@
             r_0 = resid[row]
             r = r_0 - alpha * q_0[row]
             resid[row] = r
-            keep_residual(1, row, r)
             d = r + beta * r_0
             d_1[row] = d
             states[0, row] = d
-        send_residual(1)
 
     def second_image():
         for row in range(rows):
@@ -645,6 +655,7 @@
             u_1[row] = u
             states[0, row] = u
             keep_residual(2, row, u)
+        send_residual(2, 0, 2)
 
     def last_steps():
         def vectors(row):
@@ -655,7 +666,7 @@
 
         names = ("rr", "du", "ru", "uu", "rq", "uq", "dq", "rv", "uv", "dv")
         rr, du, ru, uu, rq, uq, dq, rv, uv, dv = reduce_all(
-            1, dots(names, vectors), lambda: send_residual(2)
+            1, dots(names, vectors), lambda: send_residual(2, 2)
         )
         beta_1 = scalar(1)
         alpha = rr / du
@@ -674,13 +685,15 @@
             keep_residual(3, row, r_2 - alpha_2 * (on_u * u + on_q * q_0[row] + on_v * image[row]))
         send_residual(3)
         kept = alpha + alpha_2 * beta
-        set_scalar(2, scalar(0) + kept * beta_1)
-        set_scalar(3, kept + alpha_2)
+        on_r_1 = kept + alpha_2
+        set_scalar(2, scalar(0) + kept * beta_1 + on_r_1)
+        set_scalar(3, -scalar(0) * on_r_1)
         set_scalar(4, -alpha * alpha_2)
 
     def one_product(k, carry):
         for t in range(1, total):
             level_forward(states.at[t - 1], states.at[t], v_co)
+        pl.when(k == 0)(take_counts)
         for row in range(rows):
             adj_0[row] = wts[total - 1, row] * states[total - 1, row]
         slot = 0
@@ -752,8 +765,8 @@
         pltpu.VMEM((n_tm, rows + 2 * reach, *row), F32),
         pltpu.VMEM((2, 2, n_tm, *row), F32),
         pltpu.VMEM((2, 2, n_tm, *row), F32),
-        pltpu.VMEM((2, 2, halo, *row), F32),
-        pltpu.VMEM((2, 2, halo, *row), F32),
+        pltpu.VMEM((2, 2, halo - 1, *row), F32),
+        pltpu.VMEM((2, 2, halo - 1, *row), F32),
         pltpu.VMEM((ext, *row), F32),
         pltpu.VMEM((ext, *row), F32),
         pltpu.VMEM((ext, *row), F32),

time: 89.9 us -> 87.9 us (0.978)
  Pallas kernels: 88.9 us -> 86.9 us
    pallas_call x1, Pallas kernels: 85.3 us -> 83.3 us  [assimilate_call(): pl.pallas_call(functools.partial(assimilate_kernel, n_space, n_tm), out_s...]
where the time goes in v3:
time: 87.9 us; the launch traced here: 87.7 us
  Pallas kernels  86.9 us (99%)
    pallas_call x1, Pallas kernels, assimilate_call(): pl.pallas_call(functools.partial(assimilate_kernel, n_space, n_tm), out_s...  83.3 us
    pallas_call x1, Pallas kernels, expand_call(): pl.pallas_call(expand_kernel, in_specs=[pl.BlockSpec(memory_space=pl.ANY)...  3.61 us

profile of v3, /device:TPU:0, one launch (start us, length us, event | category | flops | bytes accessed | tf_op | source)
XLA Modules:
  0.0 87.7 jit_solution(7374590055581018513)
XLA Ops:
  0.6 83.3 %assimilate.1 = (f32[3,192,128]{2,1,0:T(8,128)}, f32[3,192,128]{2,1,0:T(8,128)}) custom-call(bf16[3,32,96,1536]{3,2,1,0:T(8,128)(2,1)} %inn.1, s32[72,384]{1,0:T(8,128)} %bitcast.9, f32[768,384]{1,0:T(8,128)} %bitcast.5, f32[768,384]{1,0:T(8,128)} %bitcast.6), custom_call_target="tpu_custom_call" | custom-call | tf_op jit(solution)/shard_map/assimilate/pallas_call | solution.py:808
  83.9 3.6 %expand.1 = (f32[8,96,1536]{2,1,0:T(8,128)}, f32[8,24,384]{2,1,0:T(8,128)}) custom-call(f32[3,8,24,128]{3,2,1,0:T(8,128)} %bitcast.7, f32[3,8,24,128]{3,2,1,0:T(8,128)} %bitcast.8), custom_call_target="tpu_custom_call" | custom-call | tf_op jit(solution)/shard_map/expand/pallas_call | solution.py:877
